TPU v7x, 64 devices: a 2x2x8 block of a 4x4x8 slice. The times are simulated.
64 devices in a mesh: dp: 4 (over x, y), fsdp: 16 (over z, core).
Axes of the slice: x: 2, y: 2, z: 8, core: 2. Of those that a mesh axis runs over, the one named last changes fastest.
The devices are a block of a 4x4x8 slice.
Arguments:
- tokens: int32 [64, 128], P(('dp', 'fsdp')), parts along dimension 0
- embed_table: bfloat16 [128256, 2048], P('fsdp')
- norm_attn: bfloat16 [2048], P('fsdp')
- w_qkv: bfloat16 [2048, 3072], P('fsdp')
- w_out: bfloat16 [2048, 2048], P('fsdp')
- norm_mlp: bfloat16 [2048], P('fsdp')
- w_gate_up: bfloat16 [2048, 16384], P('fsdp')
- w_down: bfloat16 [8192, 2048], P('fsdp')
- rope_scale: float32 [32], replicated
Outputs:
- output 1: bfloat16 [64, 128, 2048], P(('dp', 'fsdp')), parts along dimension 0
- output 2: bfloat16 [64, 128, 8, 64], P(('dp', 'fsdp')), parts along dimension 0
- output 3: bfloat16 [64, 128, 8, 64], P(('dp', 'fsdp')), parts along dimension 0
There are 4 independent parts. A program takes and returns all parts, laid end to end along the dimension named above; an argument that names none is the same for every part.
All inputs are finite; a program needn't handle non-finite values.
Results may differ from a plain program's by a relative error of at most 0.0117517.
Values are sent between devices in bfloat16 or wider.
A program may use at most 768 MiB of HBM per device.

v0:
```python
import jax
import jax.numpy as jnp
from jax import lax
from jax.sharding import PartitionSpec as P

NORM_EPS = 1e-5
ROPE_THETA = 10000.0


def rms_norm(hidden, gain):
    h_f32 = hidden.astype(jnp.float32)
    inv_rms = lax.rsqrt(jnp.mean(h_f32 * h_f32, axis=-1, keepdims=True) + NORM_EPS)
    return (h_f32 * inv_rms * gain.astype(jnp.float32)).astype(jnp.bfloat16)


def apply_rope(proj, rope_scale):
    seq_len = proj.shape[1]
    head_dim = proj.shape[-1]
    half_dim = head_dim // 2
    freq_expo = jnp.arange(half_dim, dtype=jnp.float32) * (2.0 / head_dim)
    inv_freq = 1.0 / (rope_scale * jnp.power(ROPE_THETA, freq_expo))
    angles = jnp.arange(seq_len, dtype=jnp.float32)[:, None] * inv_freq[None, :]
    cos_tab = jnp.cos(angles)[:, None, :]
    sin_tab = jnp.sin(angles)[:, None, :]
    low_half = proj[..., :half_dim]
    high_half = proj[..., half_dim:]
    return jnp.concatenate([low_half * cos_tab - high_half * sin_tab, high_half * cos_tab + low_half * sin_tab], axis=-1)


def decoder_layer(hidden, norm_attn, w_qkv, w_out, norm_mlp, w_gate_up, w_down, rope_scale):
    n_seq = hidden.shape[0]
    seq_len = hidden.shape[1]
    head_dim = 2 * rope_scale.shape[0]
    q_width = w_out.shape[0]
    kv_width = (w_qkv.shape[1] - q_width) // 2
    n_heads = q_width // head_dim
    kv_heads = kv_width // head_dim
    ff_width = w_down.shape[0]
    normed = rms_norm(hidden, norm_attn)
    qkv_proj = jnp.einsum('bld,de->ble', normed, w_qkv, preferred_element_type=jnp.float32)
    query_rot = apply_rope(qkv_proj[..., :q_width].reshape(n_seq, seq_len, n_heads, head_dim), rope_scale).astype(jnp.bfloat16)
    key_rot = apply_rope(qkv_proj[..., q_width:q_width + kv_width].reshape(n_seq, seq_len, kv_heads, head_dim), rope_scale).astype(jnp.bfloat16)
    values = qkv_proj[..., q_width + kv_width:].reshape(n_seq, seq_len, kv_heads, head_dim).astype(jnp.bfloat16)
    q_grouped = query_rot.reshape(n_seq, seq_len, kv_heads, n_heads // kv_heads, head_dim)
    scores = jnp.einsum('bqkgd,bskd->bkgqs', q_grouped, key_rot, preferred_element_type=jnp.float32) * (head_dim ** -0.5)
    causal = jnp.arange(seq_len)[:, None] >= jnp.arange(seq_len)[None, :]
    scores = jnp.where(causal, scores, -jnp.inf)
    scores = scores - jnp.max(scores, axis=-1, keepdims=True)
    weights = jnp.exp(scores)
    attn_probs = (weights / jnp.sum(weights, axis=-1, keepdims=True)).astype(jnp.bfloat16)
    context = jnp.einsum('bkgqs,bskd->bqkgd', attn_probs, values, preferred_element_type=jnp.float32)
    context = context.astype(jnp.bfloat16).reshape(n_seq, seq_len, q_width)
    attn_proj = jnp.einsum('ble,ed->bld', context, w_out, preferred_element_type=jnp.float32)
    resid_mid = (hidden.astype(jnp.float32) + attn_proj).astype(jnp.bfloat16)
    normed_mlp = rms_norm(resid_mid, norm_mlp)
    gate_up = jnp.einsum('bld,df->blf', normed_mlp, w_gate_up, preferred_element_type=jnp.float32)
    mlp_act = (jax.nn.silu(gate_up[..., :ff_width]) * gate_up[..., ff_width:]).astype(jnp.bfloat16)
    down_proj = jnp.einsum('blf,fd->bld', mlp_act, w_down, preferred_element_type=jnp.float32)
    layer_out = (resid_mid.astype(jnp.float32) + down_proj).astype(jnp.bfloat16)
    return layer_out, key_rot, values


def gather_rows(weight):
    return lax.all_gather(weight, 'fsdp', axis=0, tiled=True)


def solution(mesh):
    batch_axes = ('dp', 'fsdp')
    row_spec = P('fsdp', None)

    def device_step(tokens, embed_table, norm_attn, w_qkv, w_out, norm_mlp, w_gate_up, w_down, rope_scale):
        group_tokens = lax.all_gather(tokens, 'fsdp', axis=0, tiled=True)
        shard_rows = embed_table.shape[0]
        local_ids = group_tokens - lax.axis_index('fsdp') * shard_rows
        owned_mask = (local_ids >= 0) & (local_ids < shard_rows)
        table_rows = jnp.take(embed_table, jnp.clip(local_ids, 0, shard_rows - 1), axis=0)
        table_rows = jnp.where(owned_mask[..., None], table_rows, jnp.zeros((), table_rows.dtype))
        hidden = lax.psum_scatter(table_rows, 'fsdp', scatter_dimension=0, tiled=True)
        full_norm_attn = gather_rows(norm_attn)
        full_qkv = gather_rows(w_qkv)
        full_out = gather_rows(w_out)
        full_norm_mlp = gather_rows(norm_mlp)
        full_gate_up = gather_rows(w_gate_up)
        full_down = gather_rows(w_down)
        return decoder_layer(hidden, full_norm_attn, full_qkv, full_out, full_norm_mlp, full_gate_up, full_down, rope_scale)

    return jax.shard_map(
        device_step,
        mesh=mesh,
        in_specs=(P(batch_axes, None), row_spec, P('fsdp'), row_spec, row_spec, P('fsdp'), row_spec, row_spec, P(None)),
        out_specs=(P(batch_axes, None, None), P(batch_axes, None, None, None), P(batch_axes, None, None, None)),
        check_vma=False,
    )
```

profile of v0, /device:TPU:21, one launch (start us, length us, event | category | flops | bytes accessed | tf_op | source)
XLA Modules:
  0.0 863.8 jit_solution(14537296865124699275)
XLA Ops:
  7.2 0.1 reduce-scatter.2.cloned.1.call-start
  7.2 22.8 %all-gather = s32[16,1,128]{2,1,0:T(1,128)S(1)} all-gather(s32[1,1,128]{2,1,0:T(1,128)} %bitcast.96), channel_id=1, replica_groups=mesh['dp'=4,'fsdp'=16] {'fsdp'}, dimensions={0}, use_global_device_ids=true | all-gather | bytes 8704 | tf_op jit(solution)/shard_map/all_gather | solution.py:72
  30.1 100.7 %gather_fusion = bf16[2048,2048]{1,0:T(8,128)(2,1)} fusion(bf16[8016,2048]{1,0:T(8,128)(2,1)} %param.10, s32[2048]{0:T(1024)S(1)} %bitcast_clamp_fusion), kind=kCustom, calls=%fused_computation | custom fusion | bytes 16785408 | tf_op jit(solution)/shard_map/jit(_take)/gather | solution.py:76
  130.7 7.4 select_select_fusion
  138.1 0.1 reduce-scatter.2.cloned.1.call-update
  138.2 0.0 copy-start.2
  138.2 0.0 copy-start.3
  138.2 0.0 copy-start.4
  138.2 0.1 all-gather.8.cloned.1.call-start
  138.3 0.7 all-gather.8.cloned.1.call-update
  139.0 0.1 all-gather.10.cloned.1.call-start
  139.1 0.7 all-gather.10.cloned.1.call-update
  139.8 0.1 all-gather.12.cloned.1.call-start
  139.9 0.6 all-gather.12.cloned.1.call-update
  140.5 0.1 all-gather.14.cloned.1.call-start
  140.5 0.6 all-gather.14.cloned.1.call-update
  141.1 0.0 copy-done.2
  141.1 23.1 %all-gather.1 = bf16[16,1,128]{2,1,0:T(2,128)(2,1)S(1)} all-gather(bf16[1,1,128]{2,1,0:T(2,128)(2,1)S(1)} %bitcast.97), channel_id=1, replica_groups=mesh['dp'=4,'fsdp'=16] {'fsdp'}, dimensions={0}, use_global_device_ids=true | all-gather | bytes 4352 | tf_op jit(solution)/shard_map/all_gather | solution.py:64
  164.3 0.0 copy-done.3
  164.3 14.9 %all-gather.2 = bf16[16,1,128]{2,1,0:T(2,128)(2,1)S(1)} all-gather(bf16[1,1,128]{2,1,0:T(2,128)(2,1)S(1)} %bitcast.98), channel_id=1, replica_groups=mesh['dp'=4,'fsdp'=16] {'fsdp'}, dimensions={0}, use_global_device_ids=true | all-gather | bytes 4352 | tf_op jit(solution)/shard_map/all_gather | solution.py:64
  179.3 0.0 copy-done.4
  179.3 0.1 fusion.27
  179.5 30.2 %reduce-scatter.2.cloned.1.call-done = bf16[1,128,2048]{2,1,0:T(8,128)(2,1)} async-done(((bf16[16,128,2048]{2,1,0:T(8,128)(2,1)}), bf16[1,128,2048]{2,1,0:T(8,128)(2,1)}) %reduce-scatter.2.cloned.1.call-update) | async-done | bytes 524304 | tf_op jit(solution)/shard_map/reduce_scatter | solution.py:78
  209.6 1.2 fusion.9
  210.8 74.9 %all-gather.8.cloned.1.call-done = bf16[2048,3072]{1,0:T(8,128)(2,1)} async-done(((bf16[128,3072]{1,0:T(8,128)(2,1)}), bf16[2048,3072]{1,0:T(8,128)(2,1)}) %all-gather.8.cloned.1.call-update) | async-done | bytes 12582928 | tf_op jit(solution)/shard_map/all_gather | solution.py:64
  285.7 6.7 convolution_bitcast_fusion.1
  292.4 0.1 slice.42
  292.5 0.1 copy.28
  292.7 0.3 copy.29
  293.0 0.1 copy.27
  293.1 0.0 copy-start.1
  293.2 0.7 pad_maximum_fusion
  293.9 0.1 subtract_convert_fusion
  294.0 0.5 fusion.30
  294.5 0.4 fusion.8
  294.9 0.0 copy-start
  294.9 0.6 convolution_convert_fusion
  295.5 0.0 copy-done.1
  295.5 42.9 %all-gather.10.cloned.1.call-done = bf16[2048,2048]{1,0:T(8,128)(2,1)} async-done(((bf16[128,2048]{1,0:T(8,128)(2,1)}), bf16[2048,2048]{1,0:T(8,128)(2,1)}) %all-gather.10.cloned.1.call-update) | async-done | bytes 8388624 | tf_op jit(solution)/shard_map/all_gather | solution.py:64
  338.4 0.0 copy-done
  338.4 4.7 multiply_reduce_fusion
  343.2 324.4 %all-gather.12.cloned.1.call-done = bf16[2048,16384]{1,0:T(8,128)(2,1)} async-done(((bf16[128,16384]{1,0:T(8,128)(2,1)}), bf16[2048,16384]{1,0:T(8,128)(2,1)}) %all-gather.12.cloned.1.call-update) | async-done | bytes 67108880 | tf_op jit(solution)/shard_map/all_gather | solution.py:64
  667.6 26.2 %convolution_bitcast_fusion = f32[1,128,16384]{2,1,0:T(8,128)} fusion(bf16[2048,16384]{1,0:T(8,128)(2,1)} %all-gather.12.cloned.1.call-done, f32[1,128,2048]{2,1,0:T(8,128)S(1)} %get-tuple-element.15, f32[2048]{0:T(1024)S(1)} %bitcast.85, f32[128]{0:T(128)S(1)} %add_rsqrt_fusion), kind=kOutput, calls=%fused_computation.1 | convolution fusion | flops 8590721024 | bytes 76554752 | tf_op jit(solution)/shard_map/bld,df->blf/dot_general | solution.py:56
  693.8 144.9 %all-gather.14.cloned.1.call-done = bf16[8192,2048]{1,0:T(8,128)(2,1)} async-done(((bf16[512,2048]{1,0:T(8,128)(2,1)}), bf16[8192,2048]{1,0:T(8,128)(2,1)}) %all-gather.14.cloned.1.call-update) | async-done | bytes 33554448 | tf_op jit(solution)/shard_map/all_gather | solution.py:64
  838.6 18.6 %fusion.5 = bf16[1,128,2048]{2,1,0:T(8,128)(2,1)} fusion(f32[1,128,2048]{2,1,0:T(8,128)S(1)} %get-tuple-element.15, bf16[8192,2048]{1,0:T(8,128)(2,1)} %all-gather.14.cloned.1.call-done, f32[1,128,16384]{2,1,0:T(8,128)} %convolution_bitcast_fusion), kind=kOutput, calls=%fused_computation.12 | convolution fusion | flops 4301783040 | bytes 43515904 | tf_op jit(solution)/shard_map/blf,fd->bld/dot_general | solution.py:58
  (12 shorter events, 0.2 us)
Async XLA Ops:
  7.2 202.4 %reduce-scatter.2.cloned.1.call-start = ((), (), s32[]{:S(2)}) async-start(), calls=%async_computation.1 | async-start | bytes 8912896 | tf_op jit(solution)/shard_map/reduce_scatter | solution.py:78
  138.2 2.9 copy-start.2
  138.2 26.1 %copy-start.3 = (bf16[128]{0:T(256)(128)(2,1)S(1)}, bf16[128]{0:T(256)(128)(2,1)}, u32[]{:S(2)}) copy-start(bf16[128]{0:T(256)(128)(2,1)} %param.14) | copy-start | bytes 772
  138.2 41.1 %copy-start.4 = (f32[32]{0:T(128)S(1)}, f32[32]{0:T(128)}, u32[]{:S(2)}) copy-start(f32[32]{0:T(128)} %param.17) | copy-start | bytes 388
  138.2 147.5 %all-gather.8.cloned.1.call-start = ((), (), s32[]{:S(2)}) async-start(), calls=%async_computation.2 | async-start | bytes 13369344 | tf_op jit(solution)/shard_map/all_gather | solution.py:64
  139.0 199.4 %all-gather.10.cloned.1.call-start = ((), (), s32[]{:S(2)}) async-start(), calls=%async_computation.3 | async-start | bytes 8912896 | tf_op jit(solution)/shard_map/all_gather | solution.py:64
  139.8 527.7 %all-gather.12.cloned.1.call-start = ((), (), s32[]{:S(2)}) async-start(), calls=%async_computation.4 | async-start | bytes 71303168 | tf_op jit(solution)/shard_map/all_gather | solution.py:64
  140.5 698.2 %all-gather.14.cloned.1.call-start = ((), (), s32[]{:S(2)}) async-start(), calls=%async_computation.5 | async-start | bytes 35651584 | tf_op jit(solution)/shard_map/all_gather | solution.py:64
  293.1 2.4 copy-start.1
  294.9 43.5 %copy-start = (bf16[1,128,2048]{2,1,0:T(8,128)(2,1)S(1)}, bf16[1,128,2048]{2,1,0:T(8,128)(2,1)}, u32[]{:S(2)}) copy-start(bf16[1,128,2048]{2,1,0:T(8,128)(2,1)} %reduce-scatter.2.cloned.1.call-done) | copy-start | bytes 1572868
Sparse Core Ops, SparseCore 0:
  138.3 71.2 reduce-scatter.1
  211.2 74.4 all-gather.7
  287.4 51.0 all-gather.9
  339.9 327.6 all-gather.11
  669.0 169.5 all-gather.13
where the time goes:
time: 866 us; the launch traced here: 864 us
  waiting for transfers between devices  620 us (72%)
  local copies, waits for them, and re-layouts  101 us (12%)
  blocking collectives  60.8 us (7%)
  matrix products  57.3 us (7%)
  between operations  14 us (2%)
  other arithmetic  10.1 us (1%)
    all_gather x4, waiting for transfers between devices, gather_rows(): return lax.all_gather(weight, 'fsdp', axis=0, tiled=True)  587 us
    gather x1, local copies, waits for them, and re-layouts, device_step(): jnp.take(embed_table, jnp.clip(local_ids, 0, shard_rows - 1), axis=0)  101 us
    all_gather x2, blocking collectives, gather_rows(): return lax.all_gather(weight, 'fsdp', axis=0, tiled=True)  38.1 us
    reduce_scatter x1, waiting for transfers between devices, device_step(): lax.psum_scatter(table_rows, 'fsdp', scatter_dimension=0, tiled=True)  30.2 us
    dot_general x1, matrix products, decoder_layer(): jnp.einsum('bld,df->blf', normed_mlp, w_gate_up, preferred_element_type=j...  26.2 us
    all_gather x1, blocking collectives, device_step(): group_tokens = lax.all_gather(tokens, 'fsdp', axis=0, tiled=True)  22.8 us
    dot_general x1, matrix products, decoder_layer(): jnp.einsum('blf,fd->bld', mlp_act, w_down, preferred_element_type=jnp.flo...  18.6 us
  transfers between devices with their start and end apart: 5, of which 5 were waited for; matrix products, arithmetic and copies ran while one was open for 5% of the time, Pallas kernels for 0%

commit v1 on v0

v1 whole, which is shorter than its diff:
```python
import functools
import math

import jax
import jax.numpy as jnp
from jax import lax
from jax.experimental import pallas as pl
from jax.experimental.pallas import tpu as pltpu
from jax.sharding import PartitionSpec as P

NORM_EPS = 1e-5
ROPE_THETA = 10000.0
BATCH = 32
DEPTH = 4


def gather_kernel(n_tok, gid_ref, tgt_ref, table_ref, out_ref, buf, obuf, sems, osem):
    width = table_ref.shape[2]
    n_step = n_tok // BATCH

    def fetch(step, slot):
        def one(i, carry):
            g = gid_ref[step * BATCH + i]

            @pl.when(g >= 0)
            def _():
                pltpu.make_async_copy(table_ref.at[g], buf.at[slot, i], sems.at[slot]).start()
            return carry
        lax.fori_loop(0, BATCH, one, 0, unroll=8)

    def drain(step, slot):
        def one(i, carry):
            @pl.when(gid_ref[step * BATCH + i] >= 0)
            def _():
                pltpu.make_async_copy(table_ref.at[0], buf.at[slot, 0], sems.at[slot]).wait()
            return carry
        lax.fori_loop(0, BATCH, one, 0, unroll=8)

    buf[...] = jnp.zeros_like(buf)
    for j in range(DEPTH - 1):
        fetch(j, j)

    def body(step, carry):
        slot = lax.rem(step, DEPTH)

        @pl.when(step + DEPTH - 1 < n_step)
        def _():
            fetch(step + DEPTH - 1, lax.rem(step + DEPTH - 1, DEPTH))
        drain(step, slot)
        rows = pl.ds(pl.multiple_of(step * BATCH, BATCH), BATCH)
        pick = (lax.broadcasted_iota(jnp.int32, (BATCH, BATCH * 8), 1) == tgt_ref[rows, :]).astype(jnp.bfloat16)
        block = buf[slot].reshape(BATCH * 8, width)
        got = jnp.dot(pick, block, preferred_element_type=jnp.float32)
        out_ref[rows, :] = got.astype(jnp.bfloat16)
        return carry
    lax.fori_loop(0, n_step, body, 0)


def gather_table(ids, owned, table):
    n_tok = ids.shape[0]
    n_rows, width = table.shape
    gid = jnp.where(owned, ids // 8, -1)
    lane = jnp.arange(n_tok, dtype=jnp.int32) % BATCH
    tgt = jnp.where(owned, 8 * lane + ids % 8, -1)[:, None]
    return pl.pallas_call(
        functools.partial(gather_kernel, n_tok),
        out_shape=jax.ShapeDtypeStruct((n_tok, width), jnp.bfloat16),
        in_specs=[pl.BlockSpec(memory_space=pltpu.SMEM), pl.BlockSpec(memory_space=pltpu.VMEM), pl.BlockSpec(memory_space=pl.ANY)],
        out_specs=pl.BlockSpec(memory_space=pltpu.VMEM),
        scratch_shapes=[
            pltpu.VMEM((DEPTH, BATCH, 8, width), jnp.bfloat16),
            pltpu.VMEM((8, 128), jnp.bfloat16),
            pltpu.SemaphoreType.DMA((DEPTH,)),
            pltpu.SemaphoreType.DMA,
        ],
        compiler_params=pltpu.CompilerParams(vmem_limit_bytes=48 * 2**20),
        cost_estimate=pl.CostEstimate(flops=2 * n_tok * BATCH * 8 * width, bytes_accessed=9 * n_tok * width * 2, transcendentals=0),
    )(gid, tgt, table.reshape(n_rows // 8, 8, width))


def rope_tables(seq_len, rope_scale):
    half_dim = rope_scale.shape[0]
    freq_expo = jnp.arange(half_dim, dtype=jnp.float32) * (1.0 / half_dim)
    inv_freq = 1.0 / (rope_scale * jnp.power(ROPE_THETA, freq_expo))
    angles = jnp.arange(seq_len, dtype=jnp.float32)[:, None] * inv_freq[None, :]
    return jnp.cos(angles)[:, None, :], jnp.sin(angles)[:, None, :]


def rotate(proj, cos_tab, sin_tab):
    half_dim = cos_tab.shape[-1]
    low_half = proj[..., :half_dim]
    high_half = proj[..., half_dim:]
    return jnp.concatenate([low_half * cos_tab - high_half * sin_tab, high_half * cos_tab + low_half * sin_tab], axis=-1)


def solution(mesh):
    batch_axes = ('dp', 'fsdp')
    row_spec = P('fsdp', None)
    n_dp = mesh.shape['dp']
    side = math.isqrt(n_dp)
    flip_y = [(i, i ^ 1) for i in range(n_dp)]
    flip_x = [(i, ((i // side) ^ 1) * side + i % side) for i in range(n_dp)]

    def device_step(tokens, embed_table, norm_attn, w_qkv, w_out, norm_mlp, w_gate_up, w_down, rope_scale):
        dp = lax.axis_index('dp')
        me_x = (dp // side) % 2
        me_y = dp % 2
        me = 2 * me_x + me_y
        n_fsdp = mesh.shape['fsdp']
        seq_len = tokens.shape[1]
        width = embed_table.shape[1]
        head_dim = 2 * rope_scale.shape[0]
        q_width = w_out.shape[0] * n_fsdp
        kv_width = (w_qkv.shape[1] - q_width) // 2
        ff_part = w_down.shape[0]
        q4, kv4, w4, f4 = q_width // 4, kv_width // 4, width // 4, ff_part // 4
        n_tok = 4 * seq_len

        def send_x(a):
            return lax.ppermute(a, 'dp', flip_x)

        def send_y(a):
            return lax.ppermute(a, 'dp', flip_y)

        def by_role(mine, dx, dy, dxy):
            stack = jnp.stack([mine, dy, dx, dxy])
            return stack[jnp.arange(4) ^ me]

        def square_gather(a):
            half = a.shape[0] // 2
            top, bot = a[:half], a[half:]
            top_x, bot_y = send_x(top), send_y(bot)
            top2 = send_y(jnp.concatenate([top, top_x]))
            bot2 = send_x(jnp.concatenate([bot, bot_y]))
            dx = jnp.concatenate([top_x, bot2[:half]])
            dy = jnp.concatenate([top2[:half], bot_y])
            dxy = jnp.concatenate([top2[half:], bot2[half:]])
            return by_role(a, dx, dy, dxy)

        def square_scatter(parts):
            half = parts.shape[1] // 2
            ex = parts[jnp.arange(4) ^ me]
            top, bot = ex[:, :half], ex[:, half:]
            top_r = send_x(top[2:])
            bot_r = send_y(bot[jnp.array([1, 3])])
            top1 = top[:2] + top_r
            bot1 = bot[jnp.array([0, 2])] + bot_r
            top2 = top1[0] + send_y(top1[1])
            bot2 = bot1[0] + send_x(bot1[1])
            return jnp.concatenate([top2, bot2])

        def gather_rows(weight):
            return lax.all_gather(weight, 'fsdp', axis=0, tiled=True)

        wqkv_part = jnp.concatenate([
            lax.dynamic_slice_in_dim(w_qkv, me * q4, q4, 1),
            lax.dynamic_slice_in_dim(w_qkv, q_width + me * kv4, kv4, 1),
            lax.dynamic_slice_in_dim(w_qkv, q_width + kv_width + me * kv4, kv4, 1)], axis=1)
        full_qkv = gather_rows(wqkv_part)
        full_out = gather_rows(lax.dynamic_slice_in_dim(w_out, me * w4, w4, 1))
        gains = jnp.concatenate([norm_attn[None], norm_mlp[None]])
        gains = lax.all_gather(gains, 'fsdp', axis=1, tiled=True)
        gain_attn, gain_mlp = gains[0].astype(jnp.float32), gains[1].astype(jnp.float32)

        group_tokens = lax.all_gather(tokens, 'fsdp', axis=0, tiled=True).reshape(-1)
        shard_rows = embed_table.shape[0]
        local_ids = group_tokens - lax.axis_index('fsdp') * shard_rows
        owned = (local_ids >= 0) & (local_ids < shard_rows)
        rows = gather_table(local_ids, owned, embed_table)
        hidden = lax.psum_scatter(rows.reshape(n_fsdp, seq_len, width), 'fsdp', scatter_dimension=0, tiled=False)

        gu = w_gate_up.reshape(w_gate_up.shape[0], 2 * n_fsdp, 4, f4)
        gu = lax.dynamic_index_in_dim(gu, me, 2, keepdims=False).reshape(w_gate_up.shape[0], 2 * n_fsdp * f4)
        full_gate_up = gather_rows(gu)
        full_down = gather_rows(lax.dynamic_slice_in_dim(w_down, me * f4, f4, 0))

        x_all = square_gather(hidden).reshape(n_tok, width)
        x_f32 = x_all.astype(jnp.float32)
        inv = lax.rsqrt(jnp.mean(x_f32 * x_f32, axis=-1, keepdims=True) + NORM_EPS)
        normed = (x_f32 * inv * gain_attn).astype(jnp.bfloat16)
        qkv = jnp.dot(normed, full_qkv, preferred_element_type=jnp.float32).reshape(4, seq_len, -1)
        cos_tab, sin_tab = rope_tables(seq_len, rope_scale)
        n_q, n_kv = q4 // head_dim, kv4 // head_dim
        q = rotate(qkv[..., :q4].reshape(4, seq_len, n_q, head_dim), cos_tab, sin_tab).astype(jnp.bfloat16)
        k = rotate(qkv[..., q4:q4 + kv4].reshape(4, seq_len, n_kv, head_dim), cos_tab, sin_tab).astype(jnp.bfloat16)
        v = qkv[..., q4 + kv4:].reshape(4, seq_len, n_kv, head_dim).astype(jnp.bfloat16)
        qg = q.reshape(4, seq_len, n_kv, n_q // n_kv, head_dim)
        scores = jnp.einsum('bqkgd,bskd->bkgqs', qg, k, preferred_element_type=jnp.float32) * (head_dim ** -0.5)
        causal = jnp.arange(seq_len)[:, None] >= jnp.arange(seq_len)[None, :]
        scores = jnp.where(causal, scores, -jnp.inf)
        scores = scores - jnp.max(scores, axis=-1, keepdims=True)
        weights = jnp.exp(scores)
        probs = (weights / jnp.sum(weights, axis=-1, keepdims=True)).astype(jnp.bfloat16)
        ctx = jnp.einsum('bkgqs,bskd->bqkgd', probs, v, preferred_element_type=jnp.float32)
        ctx = ctx.astype(jnp.bfloat16).reshape(n_tok, q4)

        kv = jnp.concatenate([k.reshape(4, seq_len, kv4), v.reshape(4, seq_len, kv4)], axis=-1)
        kv_ex = kv[jnp.arange(4) ^ me]
        kv_x = send_x(kv_ex[2:])
        kv_y = send_y(jnp.stack([kv_ex[1], kv_x[1]]))
        kv_all = by_role(kv_ex[0], kv_x[0], kv_y[0], kv_y[1])
        k_out = kv_all[..., :kv4].reshape(4, seq_len, n_kv, head_dim).transpose(1, 0, 2, 3).reshape(1, seq_len, 4 * n_kv, head_dim)
        v_out = kv_all[..., kv4:].reshape(4, seq_len, n_kv, head_dim).transpose(1, 0, 2, 3).reshape(1, seq_len, 4 * n_kv, head_dim)

        ctx_full = square_gather(ctx).transpose(1, 0, 2).reshape(n_tok, q_width)
        attn = jnp.dot(ctx_full, full_out, preferred_element_type=jnp.float32)
        x_cols = lax.dynamic_slice_in_dim(x_all, me * w4, w4, 1)
        mid = (x_cols.astype(jnp.float32) + attn).astype(jnp.bfloat16)
        mid_f32 = mid.astype(jnp.float32)
        ss = jnp.sum(mid_f32 * mid_f32, axis=-1, keepdims=True)
        ss = ss.reshape(4, seq_len)
        ss = ss + send_x(ss)
        ss = (ss + send_y(ss)).reshape(n_tok, 1)
        inv2 = lax.rsqrt(ss / width + NORM_EPS)
        gain_cols = lax.dynamic_slice_in_dim(gain_mlp, me * w4, w4, 0)
        h2 = (mid_f32 * inv2 * gain_cols).astype(jnp.bfloat16)
        h2_full = square_gather(h2).transpose(1, 0, 2).reshape(n_tok, width)
        gate_up = jnp.dot(h2_full, full_gate_up, preferred_element_type=jnp.float32)
        half_ff = gate_up.shape[1] // 2
        act = (jax.nn.silu(gate_up[:, :half_ff]) * gate_up[:, half_ff:]).astype(jnp.bfloat16)
        down = jnp.dot(act, full_down, preferred_element_type=jnp.float32)
        cols = lax.broadcasted_iota(jnp.int32, (1, width), 1) // w4 == me
        down = down + jnp.where(cols, jnp.tile(mid_f32, (1, 4)), 0.0)
        out = square_scatter(down.reshape(4, seq_len, width))
        return out.astype(jnp.bfloat16)[None], k_out, v_out

    return jax.shard_map(
        device_step,
        mesh=mesh,
        in_specs=(P(batch_axes, None), row_spec, P('fsdp'), row_spec, row_spec, P('fsdp'), row_spec, row_spec, P(None)),
        out_specs=(P(batch_axes, None, None), P(batch_axes, None, None, None), P(batch_axes, None, None, None)),
        check_vma=False,
    )
```

time: 866 us -> 442 us (0.51)
  waiting for transfers between devices: 620 us -> 223 us
  local copies, waits for them, and re-layouts: 101 us -> 50.7 us
  Pallas kernels: 0 us -> 41.7 us
  blocking collectives: 60.8 us -> 40.9 us
  matrix products: 57.3 us -> 39.9 us
  starting transfers between devices: 0.31 us -> 14.8 us
    all_gather x4, waiting for transfers between devices: 587 us -> 65.3 us  [gather_rows(): return lax.all_gather(weight, 'fsdp', axis=0, tiled=True)]
    ppermute x0 -> x20, waiting for transfers between devices: none -> 110 us  [the longest x10 59.4 us: send_y(): return lax.ppermute(a, 'dp', flip_y)]
    gather x1 -> x8, local copies, waits for them, and re-layouts: 101 us -> 14.7 us  [the longest x4 6.95 us: by_role(): return stack[jnp.arange(4) ^ me]]
    pallas_call x0 -> x1, Pallas kernels: none -> 41.7 us  [gather_table(): pl.pallas_call(functools.partial(gather_kernel, n_tok), out_shape=jax.Sha...]
    all_gather x3 -> x2, blocking collectives: 60.8 us -> 40.9 us  [the longest x1 22.9 us: device_step(): lax.all_gather(tokens, 'fsdp', axis=0, tiled=True).reshape(-1)]
    dot_general x6 -> x5, matrix products: 57.3 us -> 37.7 us  [the longest x1 14.6 us: device_step(): gate_up = jnp.dot(h2_full, full_gate_up, preferred_element_type=jnp.float32)]
    reduce_scatter x1, waiting for transfers between devices: 30.2 us -> 47.7 us  [device_step(): lax.psum_scatter(rows.reshape(n_fsdp, seq_len, width), 'fsdp', scatter_di...]
    ppermute x0 -> x20, starting transfers between devices: none -> 14.5 us  [the longest x10 8.86 us: send_y(): return lax.ppermute(a, 'dp', flip_y)]
  transfers between devices with their start and end apart: 5 -> 25, of which waited for: 5 -> 20; matrix products, arithmetic and copies ran while one was open for 5% -> 23% of each run, Pallas kernels for 0% -> 0%
where the time goes in v1:
time: 442 us; the launch traced here: 438 us
  waiting for transfers between devices  223 us (50%)
  local copies, waits for them, and re-layouts  50.7 us (11%)
  Pallas kernels  41.7 us (9%)
  blocking collectives  40.9 us (9%)
  matrix products  39.9 us (9%)
  starting transfers between devices  14.8 us (3%)
  between operations  14.5 us (3%)
  other arithmetic  12.4 us (3%)
    all_gather x4, waiting for transfers between devices, gather_rows(): return lax.all_gather(weight, 'fsdp', axis=0, tiled=True)  65.3 us
    ppermute x10, waiting for transfers between devices, send_y(): return lax.ppermute(a, 'dp', flip_y)  59.4 us
    ppermute x10, waiting for transfers between devices, send_x(): return lax.ppermute(a, 'dp', flip_x)  50.4 us
    reduce_scatter x1, waiting for transfers between devices, device_step(): lax.psum_scatter(rows.reshape(n_fsdp, seq_len, width), 'fsdp', scatter_di...  47.7 us
    pallas_call x1, Pallas kernels, gather_table(): pl.pallas_call(functools.partial(gather_kernel, n_tok), out_shape=jax.Sha...  41.7 us
    all_gather x1, blocking collectives, device_step(): lax.all_gather(tokens, 'fsdp', axis=0, tiled=True).reshape(-1)  22.9 us
    all_gather x1, blocking collectives, device_step(): gains = lax.all_gather(gains, 'fsdp', axis=1, tiled=True)  18 us
    dot_general x1, matrix products, device_step(): gate_up = jnp.dot(h2_full, full_gate_up, preferred_element_type=jnp.float32)  14.6 us
  transfers between devices with their start and end apart: 25, of which 20 were waited for; matrix products, arithmetic and copies ran while one was open for 23% of the time, Pallas kernels for 0%

profile of v1, /device:TPU:21, one launch (start us, length us, event | category | flops | bytes accessed | tf_op | source)
XLA Modules:
  0.0 438.1 jit_solution(14588679723591454113)
XLA Ops:
  7.3 22.9 %all-gather = s32[16,1,128]{2,1,0:T(1,128)S(1)} all-gather(s32[1,1,128]{2,1,0:T(1,128)} %bitcast.197), channel_id=1, replica_groups=mesh['dp'=4,'fsdp'=16] {'fsdp'}, dimensions={0}, use_global_device_ids=true | all-gather | bytes 8704 | tf_op jit(solution)/shard_map/all_gather | solution.py:165
  31.2 41.7 %shard_map.130 = bf16[2048,2048]{1,0:T(8,128)(2,1)} custom-call(s32[2048]{0:T(1024)S(1)} %get-tuple-element.3.gid_ref, s32[2048,1]{1,0:T(8,128)S(1)} %fusion.18.tgt_ref, bf16[1002,8,2048]{2,1,0:T(8,128)(2,1)} %bitcast.167), custom_call_target="tpu_custom_call" | custom-call | flops 2147483648 | bytes 75497472 | tf_op jit(solution)/shard_map/pallas_call | solution.py:65
  75.7 1.6 constant_dynamic-slice_fusion.2
  77.4 6.4 %copy.72 = bf16[128,16384]{0,1:T(8,128)(2,1)} copy(bf16[128,16384]{1,0:T(8,128)(2,1)} %param.17) | data formatting | bytes 8388608 | tf_op args[6]
  83.8 2.4 constant_dynamic-slice_fusion.1
  87.2 47.7 %reduce-scatter.2.cloned.1.call-done = bf16[1,128,2048]{2,1,0:T(8,128)(2,1)} async-done(((bf16[16,128,2048]{2,1,0:T(8,128)(2,1)}), bf16[1,128,2048]{2,1,0:T(8,128)(2,1)}) %reduce-scatter.2.cloned.1.call-update) | async-done | bytes 524304 | tf_op jit(solution)/shard_map/reduce_scatter | solution.py:170
  136.0 1.3 collective-permute-start
  137.3 18.0 %all_gather.19 = bf16[2,2048]{1,0:T(2,128)(2,1)S(1)} all-gather(bf16[2,128]{1,0:T(2,128)(2,1)S(1)} %pad_maximum_fusion.17), channel_id=1, replica_groups=mesh['dp'=4,'fsdp'=16] {'fsdp'}, dimensions={1}, use_global_device_ids=true | all-gather | bytes 8704 | tf_op jit(solution)/shard_map/all_gather | solution.py:162
  155.4 1.3 collective-permute-start.1
  157.3 11.6 %collective-permute-done.1 = bf16[128,2048]{1,0:T(8,128)(2,1)S(1)} collective-permute-done((bf16[128,2048]{1,0:T(8,128)(2,1)S(1)}, bf16[128,2048]{1,0:T(8,128)(2,1)S(1)}, u32[]{:S(2)}, u32[]{:S(2)}) %collective-permute-start.1) | collective-permute-done | bytes 524320 | tf_op jit(solution)/shard_map/ppermute | solution.py:123
  168.9 5.7 %collective-permute-done.2 = bf16[64,2048]{1,0:T(8,128)(2,1)S(1)} collective-permute-done((bf16[64,2048]{1,0:T(8,128)(2,1)S(1)}, bf16[64,2048]{1,0:T(8,128)(2,1)S(1)}, u32[]{:S(2)}, u32[]{:S(2)}) %collective-permute-start.2) | collective-permute-done | bytes 262176 | tf_op jit(solution)/shard_map/ppermute | solution.py:123
  175.1 12.3 %collective-permute-done.3 = bf16[128,2048]{1,0:T(8,128)(2,1)S(1)} collective-permute-done((bf16[128,2048]{1,0:T(8,128)(2,1)S(1)}, bf16[128,2048]{1,0:T(8,128)(2,1)S(1)}, u32[]{:S(2)}, u32[]{:S(2)}) %collective-permute-start.3) | collective-permute-done | bytes 524320 | tf_op jit(solution)/shard_map/ppermute | solution.py:120
  187.6 1.6 pad_maximum_fusion
  189.2 2.3 gather_fusion
  192.0 3.9 fusion.5
  197.0 2.2 fusion.81
  199.2 1.9 fusion.15
  201.8 6.1 %collective-permute-done.4 = bf16[256,512]{0,1:T(8,128)(2,1)S(1)} collective-permute-done((bf16[256,512]{0,1:T(8,128)(2,1)S(1)}, bf16[256,512]{0,1:T(8,128)(2,1)S(1)}, u32[]{:S(2)}, u32[]{:S(2)}) %collective-permute-start.4) | collective-permute-done | bytes 262176 | tf_op jit(solution)/shard_map/ppermute | solution.py:120
  209.9 9.2 %collective-permute-done.5 = bf16[512,512]{0,1:T(8,128)(2,1)S(1)} collective-permute-done((bf16[512,512]{0,1:T(8,128)(2,1)S(1)}, bf16[512,512]{0,1:T(8,128)(2,1)S(1)}, u32[]{:S(2)}, u32[]{:S(2)}) %collective-permute-start.5) | collective-permute-done | bytes 524320 | tf_op jit(solution)/shard_map/ppermute | solution.py:123
  219.1 5.7 %collective-permute-done.6 = bf16[256,512]{0,1:T(8,128)(2,1)S(1)} collective-permute-done((bf16[256,512]{0,1:T(8,128)(2,1)S(1)}, bf16[256,512]{0,1:T(8,128)(2,1)S(1)}, u32[]{:S(2)}, u32[]{:S(2)}) %collective-permute-start.6) | collective-permute-done | bytes 262176 | tf_op jit(solution)/shard_map/ppermute | solution.py:123
  225.8 9.8 %collective-permute-done.7 = bf16[512,512]{0,1:T(8,128)(2,1)} collective-permute-done((bf16[512,512]{0,1:T(8,128)(2,1)S(1)}, bf16[512,512]{0,1:T(8,128)(2,1)}, u32[]{:S(2)}, u32[]{:S(2)}) %collective-permute-start.7) | collective-permute-done | bytes 524320 | tf_op jit(solution)/shard_map/ppermute | solution.py:120
  237.0 2.1 gather_fusion.1
  239.1 3.7 multiply_reduce_fusion
  242.9 2.8 collective-permute-done.8
  246.0 2.6 collective-permute-done.9
  248.9 5.6 %collective-permute-done.10 = bf16[256,512]{1,0:T(8,128)(2,1)S(1)} collective-permute-done((bf16[256,512]{1,0:T(8,128)(2,1)S(1)}, bf16[256,512]{1,0:T(8,128)(2,1)S(1)}, u32[]{:S(2)}, u32[]{:S(2)}) %collective-permute-start.10) | collective-permute-done | bytes 262176 | tf_op jit(solution)/shard_map/ppermute | solution.py:120
  256.1 6.6 %collective-permute-done.11 = bf16[512,512]{1,0:T(8,128)(2,1)S(1)} collective-permute-done((bf16[512,512]{1,0:T(8,128)(2,1)S(1)}, bf16[512,512]{1,0:T(8,128)(2,1)S(1)}, u32[]{:S(2)}, u32[]{:S(2)}) %collective-permute-start.11) | collective-permute-done | bytes 524320 | tf_op jit(solution)/shard_map/ppermute | solution.py:123
  262.7 5.0 %collective-permute-done.12 = bf16[256,512]{1,0:T(8,128)(2,1)S(1)} collective-permute-done((bf16[256,512]{1,0:T(8,128)(2,1)S(1)}, bf16[256,512]{1,0:T(8,128)(2,1)S(1)}, u32[]{:S(2)}, u32[]{:S(2)}) %collective-permute-start.12) | collective-permute-done | bytes 262176 | tf_op jit(solution)/shard_map/ppermute | solution.py:123
  269.4 1.6 collective-permute-start.18
  271.7 4.0 copy.81
  278.5 2.0 gather_fusion.2
  280.5 2.8 copy.71
  283.3 27.6 %all-gather.10.cloned.1.call-done = bf16[2048,4096]{0,1:T(8,128)(2,1)} async-done(((bf16[128,4096]{0,1:T(8,128)(2,1)}), bf16[2048,4096]{0,1:T(8,128)(2,1)}) %all-gather.10.cloned.1.call-update) | async-done | bytes 16777232 | tf_op jit(solution)/shard_map/all_gather | solution.py:153
  310.8 14.6 %fusion.86 = f32[512,4096]{1,0:T(8,128)} fusion(bf16[512,2048]{0,1:T(8,128)(2,1)S(1)} %bitcast.177, bf16[2048,4096]{0,1:T(8,128)(2,1)} %all-gather.10.cloned.1.call-done), kind=kOutput, calls=%fused_computation.165 | convolution fusion | flops 8589934592 | bytes 27262976 | tf_op jit(solution)/shard_map/dot_general | solution.py:218
  325.5 37.7 %all-gather.12.cloned.1.call-done = bf16[2048,2048]{1,0:T(8,128)(2,1)} async-done(((bf16[128,2048]{1,0:T(8,128)(2,1)}), bf16[2048,2048]{1,0:T(8,128)(2,1)}) %all-gather.12.cloned.1.call-update) | async-done | bytes 8388624 | tf_op jit(solution)/shard_map/all_gather | solution.py:153
  363.2 13.6 %select_add_fusion = f32[512,2048]{1,0:T(8,128)} fusion(f32[512,2048]{1,0:T(8,128)} %bitcast.174, bf16[2048,2048]{1,0:T(8,128)(2,1)} %all-gather.12.cloned.1.call-done, f32[512,4096]{1,0:T(8,128)} %fusion.86, pred[2048]{0:T(1024)(128)(4,1)S(1)} %fusion.54), kind=kOutput, calls=%fused_computation.16 | convolution fusion | flops 4303355904 | bytes 25167872 | tf_op jit(solution)/shard_map/dot_general | solution.py:221
  376.8 5.0 %gather_fusion.3 = f32[4,128,2048]{2,1,0:T(8,128)} fusion(f32[4,128,2048]{2,1,0:T(8,128)} %bitcast.175, s32[1024]{0:T(1024)S(1)} %pad_clamp_fusion.2), kind=kCustom, calls=%fused_computation.3 | custom fusion | bytes 8388624 | tf_op jit(solution)/shard_map/gather | solution.py:142
  381.8 2.4 slice.245
  385.4 1.3 collective-permute-start.19
  386.7 3.4 collective-permute-done.19
  390.1 1.8 slice.248
  391.9 1.6 gather_fusion.5
  396.0 12.7 %collective-permute-done.14 = f32[2,64,2048]{2,1,0:T(8,128)} collective-permute-done((f32[2,64,2048]{2,1,0:T(8,128)}, f32[2,64,2048]{2,1,0:T(8,128)}, u32[]{:S(2)}, u32[]{:S(2)}) %collective-permute-start.14) | collective-permute-done | bytes 1048608 | tf_op jit(solution)/shard_map/ppermute | solution.py:120
  408.7 1.7 slice_add_fusion
  412.5 4.6 %collective-permute-done.16 = f32[2,64,2048]{2,1,0:T(8,128)} collective-permute-done((f32[2,64,2048]{2,1,0:T(8,128)}, f32[2,64,2048]{2,1,0:T(8,128)}, u32[]{:S(2)}, u32[]{:S(2)}) %collective-permute-start.16) | collective-permute-done | bytes 1048608 | tf_op jit(solution)/shard_map/ppermute | solution.py:123
  417.1 1.3 add.181
  420.6 1.8 copy.74
  423.2 5.1 %collective-permute-done.15 = f32[64,2048]{1,0:T(8,128)} collective-permute-done((f32[64,2048]{1,0:T(8,128)}, f32[64,2048]{1,0:T(8,128)}, u32[]{:S(2)}, u32[]{:S(2)}) %collective-permute-start.15) | collective-permute-done | bytes 524320 | tf_op jit(solution)/shard_map/ppermute | solution.py:123
  (135 shorter events, 33.2 us)
Async XLA Ops:
  7.2 79.1 %copy-start = (bf16[512,2048]{1,0:T(8,128)(2,1)S(1)}, bf16[512,2048]{1,0:T(8,128)(2,1)}, u32[]{:S(2)}) copy-start(bf16[512,2048]{1,0:T(8,128)(2,1)} %param.18) | copy-start | bytes 6291460
  7.2 127.7 %reduce-scatter.2.cloned.1.call-start = ((), (), s32[]{:S(2)}) async-start(), calls=%async_computation.1 | async-start | bytes 8912896 | tf_op jit(solution)/shard_map/reduce_scatter | solution.py:170
  73.0 119.0 %all-gather.6.cloned.1.call-start = ((), (), s32[]{:S(2)}) async-start(), calls=%async_computation.2 | async-start | bytes 3342336 | tf_op jit(solution)/shard_map/all_gather | solution.py:153
  75.6 163.5 %all-gather.8.cloned.1.call-start = ((), (), s32[]{:S(2)}) async-start(), calls=%async_computation.3 | async-start | bytes 2228224 | tf_op jit(solution)/shard_map/all_gather | solution.py:153
  77.3 233.5 %all-gather.10.cloned.1.call-start = ((), (), s32[]{:S(2)}) async-start(), calls=%async_computation.4 | async-start | bytes 17825792 | tf_op jit(solution)/shard_map/all_gather | solution.py:153
  86.1 51.2 %copy-start.8 = (bf16[128]{0:T(256)(128)(2,1)S(1)}, bf16[128]{0:T(256)(128)(2,1)}, u32[]{:S(2)}) copy-start(bf16[128]{0:T(256)(128)(2,1)} %param.16) | copy-start | bytes 772
  86.1 51.2 %copy-start.9 = (bf16[128]{0:T(256)(128)(2,1)S(1)}, bf16[128]{0:T(256)(128)(2,1)}, u32[]{:S(2)}) copy-start(bf16[128]{0:T(256)(128)(2,1)} %param.13) | copy-start | bytes 772
  86.2 70.5 %copy-start.10 = (f32[32]{0:T(128)S(1)}, f32[32]{0:T(128)}, u32[]{:S(2)}) copy-start(f32[32]{0:T(128)} %param.19) | copy-start | bytes 388
  86.2 277.0 %all-gather.12.cloned.1.call-start = ((), (), s32[]{:S(2)}) async-start(), calls=%async_computation.5 | async-start | bytes 8912896 | tf_op jit(solution)/shard_map/all_gather | solution.py:153
  136.0 19.4 %collective-permute-start = (bf16[64,2048]{1,0:T(8,128)(2,1)S(1)}, bf16[64,2048]{1,0:T(8,128)(2,1)S(1)}, u32[]{:S(2)}, u32[]{:S(2)}) collective-permute-start(bf16[64,2048]{1,0:T(8,128)(2,1)S(1)} %get-tuple-element.25), channel_id=1, source_target_pairs={{0,32},{16,48},{32,0},{48,16},{1,33},{17,49},{33,1},{49,17},{2,34}... | collective-permute-start | bytes 786440 | tf_op jit(solution)/shard_map/ppermute | solution.py:120
  155.4 13.4 %collective-permute-start.1 = (bf16[128,2048]{1,0:T(8,128)(2,1)S(1)}, bf16[128,2048]{1,0:T(8,128)(2,1)S(1)}, u32[]{:S(2)}, u32[]{:S(2)}) collective-permute-start(bf16[128,2048]{1,0:T(8,128)(2,1)S(1)} %pad_maximum_fusion.9), channel_id=1, source_target_pairs={{0,16},{16,0},{32,48},{48,32},{1,17},{17,1},{33,49},{49,33},{2,18}... | collective-permute-start | bytes 1572872 | tf_op jit(solution)/shard_map/ppermute | solution.py:123
  156.9 17.7 %collective-permute-start.2 = (bf16[64,2048]{1,0:T(8,128)(2,1)S(1)}, bf16[64,2048]{1,0:T(8,128)(2,1)S(1)}, u32[]{:S(2)}, u32[]{:S(2)}) collective-permute-start(bf16[64,2048]{1,0:T(8,128)(2,1)S(1)} %get-tuple-element.26), channel_id=1, source_target_pairs={{0,16},{16,0},{32,48},{48,32},{1,17},{17,1},{33,49},{49,33},{2,18}... | collective-permute-start | bytes 786440 | tf_op jit(solution)/shard_map/ppermute | solution.py:123
  174.6 13.0 %copy-start.6 = (bf16[1,128,2048]{2,1,0:T(8,128)(2,1)S(1)}, bf16[1,128,2048]{2,1,0:T(8,128)(2,1)}, u32[]{:S(2)}) copy-start(bf16[1,128,2048]{2,1,0:T(8,128)(2,1)} %reduce-scatter.2.cloned.1.call-done) | copy-start | bytes 1572868
  174.7 12.8 %collective-permute-start.3 = (bf16[128,2048]{1,0:T(8,128)(2,1)S(1)}, bf16[128,2048]{1,0:T(8,128)(2,1)S(1)}, u32[]{:S(2)}, u32[]{:S(2)}) collective-permute-start(bf16[128,2048]{1,0:T(8,128)(2,1)S(1)} %get-tuple-element.38), channel_id=1, source_target_pairs={{0,32},{16,48},{32,0},{48,16},{1,33},{17,49},{33,1},{49,17},{2,34}... | collective-permute-start | bytes 1572872 | tf_op jit(solution)/shard_map/ppermute | solution.py:120
  191.5 4.5 %copy-start.2 = (bf16[4,128,2048]{2,1,0:T(8,128)(2,1)}, bf16[4,128,2048]{2,1,0:T(8,128)(2,1)S(1)}, u32[]{:S(2)}) copy-start(bf16[4,128,2048]{2,1,0:T(8,128)(2,1)S(1)} %gather_fusion) | copy-start | bytes 6291460
  201.4 6.4 %collective-permute-start.4 = (bf16[256,512]{0,1:T(8,128)(2,1)S(1)}, bf16[256,512]{0,1:T(8,128)(2,1)S(1)}, u32[]{:S(2)}, u32[]{:S(2)}) collective-permute-start(bf16[256,512]{0,1:T(8,128)(2,1)S(1)} %bitcast.183), channel_id=1, source_target_pairs={{0,32},{16,48},{32,0},{48,16},{1,33},{17,49},{33,1},{49,17},{2,34}... | collective-permute-start | bytes 786440 | tf_op jit(solution)/shard_map/ppermute | solution.py:120
  207.9 11.2 %collective-permute-start.5 = (bf16[512,512]{0,1:T(8,128)(2,1)S(1)}, bf16[512,512]{0,1:T(8,128)(2,1)S(1)}, u32[]{:S(2)}, u32[]{:S(2)}) collective-permute-start(bf16[512,512]{0,1:T(8,128)(2,1)S(1)} %pad_maximum_fusion.10), channel_id=1, source_target_pairs={{0,16},{16,0},{32,48},{48,32},{1,17},{17,1},{33,49},{49,33},{2,18}... | collective-permute-start | bytes 1572872 | tf_op jit(solution)/shard_map/ppermute | solution.py:123
  209.0 15.8 %collective-permute-start.6 = (bf16[256,512]{0,1:T(8,128)(2,1)S(1)}, bf16[256,512]{0,1:T(8,128)(2,1)S(1)}, u32[]{:S(2)}, u32[]{:S(2)}) collective-permute-start(bf16[256,512]{0,1:T(8,128)(2,1)S(1)} %bitcast.178), channel_id=1, source_target_pairs={{0,16},{16,0},{32,48},{48,32},{1,17},{17,1},{33,49},{49,33},{2,18}... | collective-permute-start | bytes 786440 | tf_op jit(solution)/shard_map/ppermute | solution.py:123
  224.9 10.7 %collective-permute-start.7 = (bf16[512,512]{0,1:T(8,128)(2,1)S(1)}, bf16[512,512]{0,1:T(8,128)(2,1)}, u32[]{:S(2)}, u32[]{:S(2)}) collective-permute-start(bf16[512,512]{0,1:T(8,128)(2,1)S(1)} %get-tuple-element.36), channel_id=1, source_target_pairs={{0,32},{16,48},{32,0},{48,16},{1,33},{17,49},{33,1},{49,17},{2,34}... | collective-permute-start | bytes 1572872 | tf_op jit(solution)/shard_map/ppermute | solution.py:120
  242.8 13.4 %copy-start.7 = (s32[2]{0:T(128)S(1)}, s32[2]{0:T(128)}, u32[]{:S(2)}) copy-start(s32[2]{0:T(128)} %constant.151) | copy-start | bytes 28
  242.8 2.9 collective-permute-start.8
  245.7 2.8 collective-permute-start.9
  248.8 5.7 %collective-permute-start.10 = (bf16[256,512]{1,0:T(8,128)(2,1)S(1)}, bf16[256,512]{1,0:T(8,128)(2,1)S(1)}, u32[]{:S(2)}, u32[]{:S(2)}) collective-permute-start(bf16[256,512]{1,0:T(8,128)(2,1)S(1)} %get-tuple-element.13), channel_id=1, source_target_pairs={{0,32},{16,48},{32,0},{48,16},{1,33},{17,49},{33,1},{49,17},{2,34}... | collective-permute-start | bytes 786440 | tf_op jit(solution)/shard_map/ppermute | solution.py:120
  254.6 8.1 %collective-permute-start.11 = (bf16[512,512]{1,0:T(8,128)(2,1)S(1)}, bf16[512,512]{1,0:T(8,128)(2,1)S(1)}, u32[]{:S(2)}, u32[]{:S(2)}) collective-permute-start(bf16[512,512]{1,0:T(8,128)(2,1)S(1)} %pad_maximum_fusion.11), channel_id=1, source_target_pairs={{0,16},{16,0},{32,48},{48,32},{1,17},{17,1},{33,49},{49,33},{2,18}... | collective-permute-start | bytes 1572872 | tf_op jit(solution)/shard_map/ppermute | solution.py:123
  254.9 12.8 %collective-permute-start.12 = (bf16[256,512]{1,0:T(8,128)(2,1)S(1)}, bf16[256,512]{1,0:T(8,128)(2,1)S(1)}, u32[]{:S(2)}, u32[]{:S(2)}) collective-permute-start(bf16[256,512]{1,0:T(8,128)(2,1)S(1)} %get-tuple-element.14), channel_id=1, source_target_pairs={{0,16},{16,0},{32,48},{48,32},{1,17},{17,1},{33,49},{49,33},{2,18}... | collective-permute-start | bytes 786440 | tf_op jit(solution)/shard_map/ppermute | solution.py:123
  268.6 8.4 %collective-permute-start.13 = (bf16[512,512]{1,0:T(8,128)(2,1)}, bf16[512,512]{1,0:T(8,128)(2,1)}, u32[]{:S(2)}, u32[]{:S(2)}) collective-permute-start(bf16[512,512]{1,0:T(8,128)(2,1)} %get-tuple-element.34), channel_id=1, source_target_pairs={{0,32},{16,48},{32,0},{48,16},{1,33},{17,49},{33,1},{49,17},{2,34}... | collective-permute-start | bytes 1572872 | tf_op jit(solution)/shard_map/ppermute | solution.py:120
  269.4 115.9 %collective-permute-start.18 = (bf16[2,128,256]{2,1,0:T(8,128)(2,1)S(1)}, bf16[2,128,256]{2,1,0:T(8,128)(2,1)S(1)}, u32[]{:S(2)}, u32[]{:S(2)}) collective-permute-start(bf16[2,128,256]{2,1,0:T(8,128)(2,1)S(1)} %slice.253), channel_id=1, source_target_pairs={{0,32},{16,48},{32,0},{48,16},{1,33},{17,49},{33,1},{49,17},{2,34}... | collective-permute-start | bytes 393224 | tf_op jit(solution)/shard_map/ppermute | solution.py:120
  384.1 24.6 %collective-permute-start.14 = (f32[2,64,2048]{2,1,0:T(8,128)}, f32[2,64,2048]{2,1,0:T(8,128)}, u32[]{:S(2)}, u32[]{:S(2)}) collective-permute-start(f32[2,64,2048]{2,1,0:T(8,128)} %slice.245), channel_id=1, source_target_pairs={{0,32},{16,48},{32,0},{48,16},{1,33},{17,49},{33,1},{49,17},{2,34}... | collective-permute-start | bytes 3145736 | tf_op jit(solution)/shard_map/ppermute | solution.py:120
  385.4 4.7 %collective-permute-start.19 = (bf16[2,128,256]{2,1,0:T(8,128)(2,1)S(1)}, bf16[2,128,256]{2,1,0:T(8,128)(2,1)S(1)}, u32[]{:S(2)}, u32[]{:S(2)}) collective-permute-start(bf16[2,128,256]{2,1,0:T(8,128)(2,1)S(1)} %pad_maximum_fusion.16), channel_id=1, source_target_pairs={{0,16},{16,0},{32,48},{48,32},{1,17},{17,1},{33,49},{49,33},{2,18}... | collective-permute-start | bytes 393224 | tf_op jit(solution)/shard_map/ppermute | solution.py:123
  393.6 23.5 %collective-permute-start.16 = (f32[2,64,2048]{2,1,0:T(8,128)}, f32[2,64,2048]{2,1,0:T(8,128)}, u32[]{:S(2)}, u32[]{:S(2)}) collective-permute-start(f32[2,64,2048]{2,1,0:T(8,128)} %gather_fusion.5), channel_id=1, source_target_pairs={{0,16},{16,0},{32,48},{48,32},{1,17},{17,1},{33,49},{49,33},{2,18}... | collective-permute-start | bytes 3145736 | tf_op jit(solution)/shard_map/ppermute | solution.py:123
  410.4 8.1 %copy-start.3 = (f32[2,64,2048]{2,1,0:T(8,128)}, f32[2,64,2048]{2,1,0:T(8,128)S(1)}, u32[]{:S(2)}) copy-start(f32[2,64,2048]{2,1,0:T(8,128)S(1)} %slice_add_fusion) | copy-start | bytes 3145732
  411.3 17.1 %collective-permute-start.15 = (f32[64,2048]{1,0:T(8,128)}, f32[64,2048]{1,0:T(8,128)}, u32[]{:S(2)}, u32[]{:S(2)}) collective-permute-start(f32[64,2048]{1,0:T(8,128)} %slice_bitcast_fusion.2), channel_id=1, source_target_pairs={{0,16},{16,0},{32,48},{48,32},{1,17},{17,1},{33,49},{49,33},{2,18}... | collective-permute-start | bytes 1572872 | tf_op jit(solution)/shard_map/ppermute | solution.py:123
  418.4 1.2 copy-start.4
  419.6 10.0 %collective-permute-start.17 = (f32[64,2048]{1,0:T(8,128)}, f32[64,2048]{1,0:T(8,128)}, u32[]{:S(2)}, u32[]{:S(2)}) collective-permute-start(f32[64,2048]{1,0:T(8,128)} %slice_bitcast_fusion), channel_id=1, source_target_pairs={{0,32},{16,48},{32,0},{48,16},{1,33},{17,49},{33,1},{49,17},{2,34}... | collective-permute-start | bytes 1572872 | tf_op jit(solution)/shard_map/ppermute | solution.py:120
  419.9 9.7 %copy-start.5 = (f32[2,64,2048]{2,1,0:T(8,128)S(1)}, f32[2,64,2048]{2,1,0:T(8,128)}, u32[]{:S(2)}) copy-start(f32[2,64,2048]{2,1,0:T(8,128)} %copy-done.4) | copy-start | bytes 3145732
  420.6 10.9 %copy-start.1 = (bf16[512,2048]{1,0:T(8,128)(2,1)S(1)}, bf16[512,2048]{1,0:T(8,128)(2,1)}, u32[]{:S(2)}) copy-start(bf16[512,2048]{1,0:T(8,128)(2,1)} %param.18) | copy-start | bytes 6291460
Sparse Core Ops, SparseCore 0:
  73.1 61.7 reduce-scatter.1
  136.6 39.4 all-gather.5
  178.3 34.6 all-gather.7
  214.3 96.4 all-gather.9
  312.9 50.2 all-gather.11

commit v2 on v0

v2 whole, which is shorter than its diff:
```python
import functools
import math

import jax
import jax.numpy as jnp
from jax import lax
from jax.experimental import pallas as pl
from jax.experimental.pallas import tpu as pltpu
from jax.sharding import PartitionSpec as P

NORM_EPS = 1e-5
ROPE_THETA = 10000.0
PICK = 32
DEPTH = 4
LANES = 128
MESH = pl.DeviceIdType.MESH
BF16 = jnp.bfloat16
F32 = jnp.float32


def aligned(start, size, step):
    return pl.ds(pl.multiple_of(start, step), size)


class Where:
    def __init__(self, side, n_fsdp):
        self.side = side
        self.nz = n_fsdp // 2
        self.dp = lax.axis_index('dp')
        self.f = lax.axis_index('fsdp')
        self.z = self.f // 2
        self.c = self.f % 2
        self.px = self.dp // side
        self.py = self.dp % side
        self.me = 2 * (self.px % 2) + self.py % 2

    def chip(self, dz):
        return lax.rem(self.z + dz + self.nz, self.nz)

    def along_z(self, dz, core):
        return (self.dp, 2 * self.chip(dz) + core)

    def partner(self):
        return (self.dp, 2 * self.z + 1 - self.c)

    def square(self, rel, core):
        px = self.px + (1 - 2 * (self.px % 2)) if rel & 2 else self.px
        py = self.py + (1 - 2 * (self.py % 2)) if rel & 1 else self.py
        return (px * self.side + py, 2 * self.z + core)


def greet(devices):
    barrier = pltpu.get_barrier_semaphore()
    for dev in devices:
        pl.semaphore_signal(barrier, inc=1, device_id=dev, device_id_type=MESH)
    pl.semaphore_wait(barrier, len(devices))


def remote(src, dst, ssem, rsem, dev):
    return pltpu.make_async_remote_copy(src_ref=src, dst_ref=dst, send_sem=ssem, recv_sem=rsem, device_id=dev, device_id_type=MESH)


def arrived(ref, sem):
    pltpu.make_async_copy(ref, ref, sem).wait()


def ids_kernel(side, n_fsdp, tok_ref, gain_ref, ids_ref, gains_ref, lsem, ssem, rsem):
    w = Where(side, n_fsdp)
    greet([(w.dp, lax.rem(w.f + k, n_fsdp)) for k in range(1, n_fsdp)])
    own = [pltpu.make_async_copy(tok_ref, ids_ref.at[w.f], lsem.at[0]),
           pltpu.make_async_copy(gain_ref, gains_ref.at[w.f], lsem.at[1])]
    for cp in own:
        cp.start()
    sent = []
    for k in range(1, n_fsdp):
        dev = (w.dp, lax.rem(w.f + k, n_fsdp))
        for j, (src, dst) in enumerate(((tok_ref, ids_ref), (gain_ref, gains_ref))):
            cp = remote(src, dst.at[w.f], ssem.at[j, k], rsem.at[j, k], dev)
            cp.start()
            sent.append(cp)
    for cp in own:
        cp.wait()
    for cp in sent:
        cp.wait_send()
    for k in range(1, n_fsdp):
        src = lax.rem(w.f - k + n_fsdp, n_fsdp)
        arrived(ids_ref.at[src], rsem.at[0, k])
        arrived(gains_ref.at[src], rsem.at[1, k])


def gather_ids(side, n_fsdp, tokens, gains):
    return pl.pallas_call(
        functools.partial(ids_kernel, side, n_fsdp),
        out_shape=(jax.ShapeDtypeStruct((n_fsdp,) + tokens.shape, tokens.dtype), jax.ShapeDtypeStruct((n_fsdp,) + gains.shape, gains.dtype)),
        in_specs=[pl.BlockSpec(memory_space=pltpu.VMEM)] * 2,
        out_specs=(pl.BlockSpec(memory_space=pltpu.VMEM), pl.BlockSpec(memory_space=pltpu.VMEM)),
        scratch_shapes=[pltpu.SemaphoreType.DMA((2,)), pltpu.SemaphoreType.DMA((2, n_fsdp)), pltpu.SemaphoreType.DMA((2, n_fsdp))],
        compiler_params=pltpu.CompilerParams(collective_id=0, has_side_effects=True),
        name='ids',
    )(tokens, gains)


class Pieces:
    def __init__(self, rows, q4, kv4, w4, f4, n_fsdp, width):
        self.rows = rows
        self.q4, self.kv4, self.w4, self.f4 = q4, kv4, w4, f4
        self.n_fsdp = n_fsdp
        self.width = width
        self.qkv = q4 + 2 * kv4
        self.gu0 = self.qkv + w4
        self.gu_w = 2 * f4 * n_fsdp // 4
        self.dn0 = self.gu0 + 4 * self.gu_w
        self.dn_w = width // 4
        self.total = self.dn0 + width
        self.late = self.total - self.qkv
        self.chunks = [(0, self.qkv), (self.qkv, w4)]
        self.chunks += [(self.gu0 + b * self.gu_w, self.gu_w) for b in range(4)]
        self.chunks += [(self.dn0 + n * self.dn_w, self.dn_w) for n in range(4)]
        self.early = 3


def pack_copies(pc, me, pk, w_qkv, w_out, w_gu, w_dn, sem_a, sem_b):
    q4, kv4, w4, f4 = pc.q4, pc.kv4, pc.w4, pc.f4
    first = [
        (w_qkv.at[:, aligned(me * q4, q4, LANES)], pk.at[:, pl.ds(0, q4)]),
        (w_qkv.at[:, aligned(4 * q4 + me * kv4, kv4, LANES)], pk.at[:, pl.ds(q4, kv4)]),
        (w_qkv.at[:, aligned(4 * q4 + 4 * kv4 + me * kv4, kv4, LANES)], pk.at[:, pl.ds(q4 + kv4, kv4)]),
    ]
    for src, dst in first:
        pltpu.make_async_copy(src, dst, sem_a).start()
    pltpu.make_async_copy(w_out.at[:, aligned(me * w4, w4, LANES)], pk.at[:, pl.ds(pc.qkv, w4)], sem_b).start()
    ff = 4 * f4 * pc.n_fsdp
    for d in range(pc.n_fsdp):
        b, k = d // 4, d % 4
        for part in range(2):
            src = w_gu.at[:, aligned(part * ff + d * 4 * f4 + me * f4, f4, LANES)]
            dst = pk.at[:, pl.ds(pc.gu0 + b * pc.gu_w + part * (pc.gu_w // 2) + k * f4, f4)]
            pltpu.make_async_copy(src, dst, sem_b).start()
    pltpu.make_async_copy(w_dn.at[aligned(me * f4, f4, LANES), :], pk.at[:, pl.ds(pc.dn0, pc.width)], sem_b).start()


def gather_kernel(n_tok, gid_ref, tgt_ref, table_ref, out_ref, buf, obuf, sems, osem):
    width = table_ref.shape[2]
    n_step = n_tok // PICK

    def fetch(step, slot):
        def one(i, carry):
            g = gid_ref[step * PICK + i]

            @pl.when(g >= 0)
            def _():
                pltpu.make_async_copy(table_ref.at[g], buf.at[slot, i], sems.at[slot]).start()
            return carry
        lax.fori_loop(0, PICK, one, 0, unroll=8)

    def drain(step, slot):
        def one(i, carry):
            @pl.when(gid_ref[step * PICK + i] >= 0)
            def _():
                pltpu.make_async_copy(table_ref.at[0], buf.at[slot, 0], sems.at[slot]).wait()
            return carry
        lax.fori_loop(0, PICK, one, 0, unroll=8)

    buf[...] = jnp.zeros_like(buf)
    for j in range(DEPTH - 1):
        fetch(j, j)

    def body(step, carry):
        slot = lax.rem(step, DEPTH)

        @pl.when(step + DEPTH - 1 < n_step)
        def _():
            fetch(step + DEPTH - 1, lax.rem(step + DEPTH - 1, DEPTH))
        drain(step, slot)
        rows = pl.ds(pl.multiple_of(step * PICK, PICK), PICK)
        pick = (lax.broadcasted_iota(jnp.int32, (PICK, PICK * 8), 1) == tgt_ref[rows, :]).astype(jnp.bfloat16)
        block = buf[slot].reshape(PICK * 8, width)
        got = jnp.dot(pick, block, preferred_element_type=jnp.float32)
        out_ref[rows, :] = got.astype(jnp.bfloat16)
        return carry
    lax.fori_loop(0, n_step, body, 0)


def gather_table(ids, owned, table):
    n_tok = ids.shape[0]
    n_rows, width = table.shape
    gid = jnp.where(owned, ids // 8, -1)
    lane = jnp.arange(n_tok, dtype=jnp.int32) % PICK
    tgt = jnp.where(owned, 8 * lane + ids % 8, -1)[:, None]
    return pl.pallas_call(
        functools.partial(gather_kernel, n_tok),
        out_shape=jax.ShapeDtypeStruct((n_tok, width), jnp.bfloat16),
        in_specs=[pl.BlockSpec(memory_space=pltpu.SMEM), pl.BlockSpec(memory_space=pltpu.VMEM), pl.BlockSpec(memory_space=pl.ANY)],
        out_specs=pl.BlockSpec(memory_space=pltpu.VMEM),
        scratch_shapes=[
            pltpu.VMEM((DEPTH, PICK, 8, width), jnp.bfloat16),
            pltpu.VMEM((8, 128), jnp.bfloat16),
            pltpu.SemaphoreType.DMA((DEPTH,)),
            pltpu.SemaphoreType.DMA,
        ],
        compiler_params=pltpu.CompilerParams(vmem_limit_bytes=48 * 2**20),
        cost_estimate=pl.CostEstimate(flops=2 * n_tok * PICK * 8 * width, bytes_accessed=9 * n_tok * width * 2, transcendentals=0),
    )(gid, tgt, table.reshape(n_rows // 8, 8, width))


def embed_kernel(side, pc, rows_ref, w_qkv, w_out, w_gu, w_dn, x_ref, q_ref, own_ref, early_ref,
                 got, peer, rp, sb, pk, xo,
                 got_sem, pack_sem, own_sem, d2d_s, d2d_r, z_s, z_r, f_s, f_r, push_s, push_r,
                 peer_s, peer_r, rs_s, rs_r, x_s, x_r):
    n_fsdp = pc.n_fsdp
    w = Where(side, n_fsdp)
    nz = w.nz
    far = nz // 2
    seq = got.shape[2]
    hw = got.shape[3]
    width = 2 * hw
    order = [far]
    for o in range(far - 1, 0, -1):
        order += [o, -o]
    order += [0]
    mine = aligned(w.c * hw, hw, LANES)
    other = aligned((1 - w.c) * hw, hw, LANES)
    for k in range(len(order)):
        dest = w.chip(order[k])
        pltpu.make_async_copy(rows_ref.at[dest, :, :, mine], got.at[dest], got_sem.at[k]).start()
    pack_copies(pc, w.me, pk, w_qkv, w_out, w_gu, w_dn, pack_sem.at[0], pack_sem.at[1])
    greet([w.partner()] + [w.along_z(dz, core) for dz in (1, -1) for core in (0, 1)])
    dirs = (1, -1)

    for k in range(len(order)):
        dest = w.chip(order[k])
        remote(rows_ref.at[dest, :, :, other], peer.at[dest], peer_s.at[k], peer_r.at[k], w.partner()).start()

    sends = []
    arrived(pk.at[:, pl.ds(0, pc.qkv)], pack_sem.at[0])
    arrived(pk.at[:, pl.ds(pc.qkv, pc.total - pc.qkv)], pack_sem.at[1])

    def first_hop(t):
        off, cw = pc.chunks[t]
        for i, dz in enumerate(dirs):
            dst = q_ref.at[w.f] if t == 0 else early_ref.at[i, w.c, :, pl.ds(off - pc.qkv, cw)]
            cp = remote(pk.at[:, pl.ds(off, cw)], dst, z_s.at[t, i], z_r.at[t, i, w.c], w.along_z(dz, 1))
            cp.start()
            sends.append(cp)

    pk_q, pk_rest = pk.at[:, pl.ds(0, pc.qkv)], pk.at[:, pl.ds(pc.qkv, pc.late)]
    own = []
    for j, (src, dst) in enumerate(((pk_q, q_ref.at[w.f]), (pk_rest, own_ref.at[w.c]))):
        own += [pltpu.make_async_copy(src, dst, own_sem.at[j]), remote(src, dst, d2d_s.at[j], d2d_r.at[j], w.partner())]
    for cp in own:
        cp.start()


    def pair(dz):
        return q_ref.at[pl.ds(2 * w.chip(dz), 2)]

    def single(dz, i):
        return q_ref.at[pl.ds(2 * w.chip(dz) + i, 1)]

    def push(ref, i, h):
        remote(ref, ref, push_s.at[i, h], push_r, w.partner()).start()

    def forward(h):
        @pl.when(w.c == 1)
        def _():
            for i, dz in enumerate(dirs):
                if h == 1:
                    for core in range(2):
                        arrived(q_ref.at[2 * w.chip(-dz) + core], z_r.at[0, i, core])
                elif h < far:
                    arrived(pair(-dz * h), f_r.at[i, h])
                else:
                    arrived(single(-dz * h, i), f_r.at[i, h])
                if h < far - 1:
                    remote(pair(-dz * h), pair(-dz * h), f_s.at[i, h + 1], f_r.at[i, h + 1], w.along_z(dz, 1)).start()
                elif h == far - 1:
                    remote(single(-dz * h, i), single(-dz * h, i), f_s.at[i, h + 1], f_r.at[i, h + 1], w.along_z(dz, 1)).start()
                push(pair(-dz * h) if h < far else single(-dz * h, i), i, h)

    def addto(dst, terms):
        def one(r, carry):
            rows = aligned(r * 32, 32, 32)
            val = terms[0](rows)
            for term in terms[1:]:
                val = val + term(rows)
            dst(rows, val)
            return carry
        lax.fori_loop(0, seq // 32, one, 0)

    def rs_stage(k):
        o = order[k]
        dest = w.chip(o)
        arrived(got.at[dest], got_sem.at[k])
        arrived(peer.at[dest], peer_r.at[k])
        if o == 0:
            return
        for i, dz in enumerate(dirs):
            if o * dz < 0 and o != far:
                continue
            dist = abs(o)
            halves = (i,) if dist == far else (1 - i, i)
            for h in halves:
                terms = [lambda r, h=h: got[dest, h, r, :], lambda r, h=h: peer[dest, h, r, :]]
                if dist < far - 1 or (dist == far - 1 and h == i):
                    arrived(rp.at[i, dist, h], rs_r.at[i, dist, h])
                    terms.append(lambda r, h=h: rp[i, dist, h, r, :])

                def put(r, val, h=h):
                    sb[i, dist - 1, h, r, :] = val
                addto(put, terms)
                remote(sb.at[i, dist - 1, h], rp.at[i, dist - 1, h], rs_s.at[i, dist - 1, h], rs_r.at[i, dist - 1, h], w.along_z(dz, w.c)).start()

    for k in range(len(order) - 1):
        rs_stage(k)
        if k < pc.early:
            first_hop(k)
        if k >= 3:
            forward(k - 2)
    rs_stage(len(order) - 1)
    for h in range(2):
        terms = [lambda r: got[w.z, h, r, :], lambda r: peer[w.z, h, r, :]]
        for i in range(2):
            arrived(rp.at[i, 0, h], rs_r.at[i, 0, h])
            terms.append(lambda r, i=i: rp[i, 0, h, r, :])

        def put(r, val):
            xo[h, r, :] = val
        addto(put, terms)
    home = pltpu.make_async_copy(xo, x_ref.at[:, :, mine], x_s.at[1])
    away = remote(xo, x_ref.at[:, :, mine], x_s.at[0], x_r, w.partner())
    home.start()
    away.start()

    for cp in sends:
        cp.wait_send()
    for cp in own:
        cp.wait()
    for k in range(len(order)):
        dest = w.chip(order[k])
        arrived(peer.at[dest], peer_s.at[k])
    for i in range(2):
        for dist in range(1, far + 1):
            for h in ((i,) if dist == far else (0, 1)):
                arrived(sb.at[i, dist - 1, h], rs_s.at[i, dist - 1, h])

    @pl.when(w.c == 1)
    def _():
        for i, dz in enumerate(dirs):
            for t in range(1, pc.early):
                off, cw = pc.chunks[t]
                for core in range(2):
                    arrived(early_ref.at[i, core, :, pl.ds(off - pc.qkv, cw)], z_r.at[t, i, core])
            for h in range(1, far + 1):
                ref = pair(-dz * h) if h < far else single(-dz * h, i)
                arrived(ref, push_s.at[i, h])
                if h < far:
                    arrived(pair(-dz * h) if h < far - 1 else single(-dz * h, i), f_s.at[i, h + 1])

    @pl.when(w.c == 0)
    def _():
        arrived(q_ref.at[pl.ds(0, n_fsdp - 2)], push_r)
    home.wait()
    away.wait()


def embed(side, pc, rows, w_qkv, w_out, w_gu, w_dn):
    seq, width = rows.shape[2], rows.shape[3]
    nz = pc.n_fsdp // 2
    far = nz // 2
    hbm = pl.BlockSpec(memory_space=pl.ANY)
    dma = pltpu.SemaphoreType.DMA
    return pl.pallas_call(
        functools.partial(embed_kernel, side, pc),
        out_shape=(
            jax.ShapeDtypeStruct((2, seq, width), BF16),
            jax.ShapeDtypeStruct((pc.n_fsdp, pc.rows, pc.qkv), BF16),
            jax.ShapeDtypeStruct((2, pc.rows, pc.late), BF16),
            jax.ShapeDtypeStruct((2, 2, pc.rows, sum(cw for _, cw in pc.chunks[1:pc.early])), BF16)),
        in_specs=[hbm] * 5,
        out_specs=(hbm, hbm, hbm, hbm),
        scratch_shapes=[
            pltpu.VMEM((nz, 2, seq, width // 2), BF16),
            pltpu.VMEM((nz, 2, seq, width // 2), BF16),
            pltpu.VMEM((2, far, 2, seq, width // 2), BF16),
            pltpu.VMEM((2, far, 2, seq, width // 2), BF16),
            pltpu.VMEM((pc.rows, pc.total), BF16),
            pltpu.VMEM((2, seq, width // 2), BF16),
            dma((nz,)), dma((2,)), dma((2,)), dma((2,)), dma((2,)),
            dma((pc.early, 2)), dma((pc.early, 2, 2)),
            dma((2, far + 1)), dma((2, far + 1)), dma((2, far + 1)), dma,
            dma((nz,)), dma((nz,)),
            dma((2, far, 2)), dma((2, far, 2)),
            dma((2,)), dma,
        ],
        compiler_params=pltpu.CompilerParams(collective_id=1, has_side_effects=True, vmem_limit_bytes=67043328),
        name='embed',
    )(rows, w_qkv, w_out, w_gu, w_dn)


def layer_kernel(side, pc, head_dim, x_ref, q_ref, own_ref, early_ref, g1_ref, g2_ref, cos_ref, sin_ref, out_ref, k_ref, v_ref, w_ref,
                 xa, ca, xm, wg, wd, mm, pp, r1, r2, qf, kvb,
                 lsem, xs_s, xs_r, cs_s, cs_r, ms_s, ms_r, kv_s, kv_r, p1_s, p1_r, p2_s, p2_r, o_s, o_l, o_r,
                 zs, zr, ps, wch):
    h2 = ca
    n_fsdp = pc.n_fsdp
    w = Where(side, n_fsdp)
    far = w.nz // 2
    seq, width = xa.shape[2], xa.shape[3]
    rows_b = 2 * seq
    half = pc.dn_w // 2
    n_chunk = len(pc.chunks)
    last_gu = 5
    greet([w.partner(), w.along_z(1, w.c), w.along_z(-1, w.c)] + [w.square(rel, core) for rel in (1, 2, 3) for core in (0, 1)])
    dirs = (1, -1)

    def stream():
        def cols(t):
            off, cw = pc.chunks[t]
            return pl.ds(off - pc.qkv, cw)

        def pair(t, dz):
            return w_ref.at[pl.ds(2 * w.chip(dz), 2), :, cols(t)]

        def single(t, dz, i):
            return w_ref.at[pl.ds(2 * w.chip(dz) + i, 1), :, cols(t)]

        def piece(t, h, i):
            dz = dirs[i]
            return pair(t, -dz * h) if h < far else single(t, -dz * h, i)

        def source(t, h, i, ref):
            if h == 0:
                return own_ref.at[:, :, cols(t)]
            if h == 1 and t < pc.early:
                return early_ref.at[i, :, :, cols(t)]
            return ref

        sent = []

        def hop(t, h):
            if t < 1 or t >= n_chunk or (h == 0 and t < pc.early):
                return
            for i in range(2):
                dz = dirs[i]
                if h > 1 or (h == 1 and t >= pc.early):
                    arrived(piece(t, h, i), zr.at[t, i, h])
                if h < far:
                    ref = pair(t, -dz * h) if h < far - 1 else single(t, -dz * h, i)
                    remote(source(t, h, i, ref), ref, zs.at[t, i, h], zr.at[t, i, h + 1], w.along_z(dz, 1)).start()
                    sent.append((ref, zs.at[t, i, h]))
            if h > 0:
                for i in range(2):
                    ref = piece(t, h, i)
                    remote(source(t, h, i, ref), ref, ps.at[t, i, h], wch.at[t], w.partner()).start()
                    sent.append((ref, ps.at[t, i, h]))

        for s in range(pc.early - 1, n_chunk + far):
            for h in range(far + 1):
                hop(s - h, h)
        for ref, sem in sent:
            arrived(ref, sem)
        kvw = 2 * (kvb.shape[2] // 4)
        for rel in range(4):
            arrived(k_ref.at[:, pl.ds(0, kvw)], kv_r.at[rel, 0])
            arrived(v_ref.at[:, pl.ds(0, kvw)], kv_r.at[rel, 1])
        for n in range(4):
            arrived(out_ref.at[:, pl.ds(n * pc.dn_w, pc.dn_w)], o_r.at[n])

    def compute():
        y, x = w.square(1, 0), w.square(2, 0)
        q4, kv4 = pc.q4, pc.kv4
        cols = {q: aligned((w.me ^ q) * pc.w4, pc.w4, LANES) for q in range(4)}
        sent = []

        def go(cp):
            cp.start()
            sent.append(cp)

        def load(t, dst, sem):
            off, cw = pc.chunks[t]
            c = pl.ds(off - pc.qkv, cw)
            arrived(w_ref.at[pl.ds(0, n_fsdp - 2), :, c], wch.at[t])
            for dz in range(w.nz):
                two = pl.ds(2 * w.chip(dz), 2)
                src = own_ref.at[:, :, c] if dz == 0 else w_ref.at[two, :, c]
                pltpu.make_async_copy(src, dst.at[two], sem).start()

        own = pltpu.make_async_copy(x_ref, xa.at[0], lsem.at[0])
        own.start()
        first = pltpu.make_async_copy(q_ref, wg.at[:, :, pl.ds(0, pc.qkv)], lsem.at[1])
        first.start()
        go(remote(x_ref.at[0], xa.at[2, 0], xs_s.at[0], xs_r.at[2, 0], x))
        go(remote(x_ref.at[1], xa.at[1, 1], xs_s.at[1], xs_r.at[1, 1], y))
        go(remote(x_ref.at[1], xa.at[2, 1], xs_s.at[2], xs_r.at[2, 1], x))
        go(remote(x_ref.at[0], xa.at[1, 0], xs_s.at[3], xs_r.at[1, 0], y))
        own.wait()
        first.wait()

        def norm_into(dst, slot, load_rows, gain_ref):
            def one(i, carry):
                rows = aligned(i * 16, 16, 16)
                val = load_rows(rows, i).astype(F32)
                inv = lax.rsqrt(jnp.mean(val * val, axis=-1, keepdims=True) + NORM_EPS)
                dst[slot, rows, :] = (val * inv * gain_ref[...]).astype(BF16)
                return carry
            lax.fori_loop(0, rows_b // 16, one, 0)

        per = seq // 16
        lane = lax.broadcasted_iota(jnp.int32, (seq, LANES), 1)
        low_head = (lane % head_dim) < head_dim // 2
        first_head = lane < head_dim
        n_pair = q4 // LANES
        pair_per_kv = n_pair // 2

        def rope(t):
            swapped = jnp.where(low_head, pltpu.roll(t, LANES - head_dim // 2, 1), pltpu.roll(t, head_dim // 2, 1))
            return t * cos_ref[...] + swapped * sin_ref[...]

        def attend(slot):
            norm_into(mm, slot, lambda rows, i: xa[slot, i // per, aligned((i % per) * 16, 16, 16), :], g1_ref)
            def proj(nt, carry):
                c = aligned(nt * 256, 256, LANES)
                qf[:, c] = jnp.dot(mm[slot], wg[:, :, c].reshape(width, 256), preferred_element_type=F32)
                return carry
            lax.fori_loop(0, pc.qkv // 256, proj, 0)

            def one_seq(u, carry):
                rows = aligned(u * seq, seq, seq)
                k_f = rope(qf[rows, pl.ds(q4, LANES)])
                v_f = qf[rows, pl.ds(q4 + kv4, LANES)]
                kvb[slot, rows, pl.ds(0, LANES)] = k_f.astype(BF16)
                kvb[slot, rows, pl.ds(LANES, LANES)] = v_f.astype(BF16)
                k_r, v_r = pltpu.roll(k_f, head_dim, 1), pltpu.roll(v_f, head_dim, 1)
                zero = jnp.zeros_like(k_f)
                row = lax.broadcasted_iota(jnp.int32, (pair_per_kv * seq, seq), 0) % seq
                causal = row >= lax.broadcasted_iota(jnp.int32, (pair_per_kv * seq, seq), 1)
                for g in range(2):
                    k_lo, k_hi = (k_f, k_r) if g == 0 else (k_r, k_f)
                    v_lo, v_hi = (v_f, v_r) if g == 0 else (v_r, v_f)
                    kk = jnp.concatenate([jnp.where(first_head, k_lo, zero), jnp.where(first_head, zero, k_hi)], axis=0).astype(BF16)
                    vv = jnp.concatenate([jnp.where(first_head, v_lo, zero), jnp.where(first_head, zero, v_hi)], axis=0).astype(BF16)
                    qs = jnp.concatenate([rope(qf[rows, pl.ds((g * pair_per_kv + p) * LANES, LANES)]).astype(BF16) for p in range(pair_per_kv)], axis=0)
                    sc = lax.dot_general(qs, kk, (((1,), (1,)), ((), ())), preferred_element_type=F32) * (head_dim ** -0.5)
                    probs = []
                    for e in range(2):
                        part = jnp.where(causal, sc[:, e * seq:(e + 1) * seq], -jnp.inf)
                        part = jnp.exp(part - jnp.max(part, axis=-1, keepdims=True))
                        probs.append((part / jnp.sum(part, axis=-1, keepdims=True)).astype(BF16))
                    ctx = jnp.dot(jnp.concatenate(probs, axis=1), vv, preferred_element_type=F32).astype(BF16)
                    for p in range(pair_per_kv):
                        lanes = aligned(w.me * pc.w4 + (g * pair_per_kv + p) * LANES, LANES, LANES)
                        ca[slot, rows, lanes] = ctx[p * seq:(p + 1) * seq]
                return carry
            lax.fori_loop(0, 2, one_seq, 0)

        def spread(buf, slot, ss, rs):
            mine = buf.at[slot, :, cols[0]]
            go(remote(mine, buf.at[slot ^ 2, :, cols[0]], ss.at[slot, 1], rs.at[slot ^ 2, 1], x))
            go(remote(mine, buf.at[slot ^ 1, :, cols[0]], ss.at[slot, 0], rs.at[slot ^ 1, 0], y))

        def take(buf, slot, q, rs):
            arrived(buf.at[slot, :, cols[q]], rs.at[slot, q - 1 if q < 3 else 2])

        def relay(buf, slot, q, ss, rs):
            take(buf, slot, q, rs)
            ref = buf.at[slot, :, cols[q]]
            to, dev = (slot ^ 1, y) if q == 2 else (slot ^ 2, x)
            go(remote(ref, buf.at[to, :, cols[q]], ss.at[to, 2], rs.at[to, 2], dev))

        def send_kv(slot):
            mine = aligned(w.me * kv4, kv4, LANES)
            for core in range(2):
                for j, dst in enumerate((k_ref, v_ref)):
                    src = kvb.at[slot, pl.ds(core * seq, seq), pl.ds(j * kv4, kv4)]
                    if slot == 0 and core == 0:
                        cp = pltpu.make_async_copy(src, dst.at[:, mine], kv_s.at[slot, core, j])
                        cp.start()
                        local_kv.append(cp)
                    else:
                        go(remote(src, dst.at[:, mine], kv_s.at[slot, core, j], kv_r.at[slot, j], w.square(slot, core)))
        local_kv = []

        def here(slot, h):
            arrived(xa.at[slot, h], xs_r.at[slot, h])

        attend(0)
        here(2, 0)
        go(remote(xa.at[2, 0], xa.at[3, 0], xs_s.at[4], xs_r.at[3, 0], y))
        here(1, 1)
        go(remote(xa.at[1, 1], xa.at[3, 1], xs_s.at[5], xs_r.at[3, 1], x))
        spread(ca, 0, cs_s, cs_r)
        here(2, 1)
        attend(2)
        spread(ca, 2, cs_s, cs_r)
        here(1, 0)
        attend(1)
        spread(ca, 1, cs_s, cs_r)
        relay(ca, 2, 2, cs_s, cs_r)
        here(3, 0)
        here(3, 1)
        attend(3)
        spread(ca, 3, cs_s, cs_r)
        relay(ca, 0, 2, cs_s, cs_r)
        relay(ca, 0, 1, cs_s, cs_r)
        relay(ca, 2, 1, cs_s, cs_r)
        load(1, wd, lsem.at[0])
        for slot in range(4):
            send_kv(slot)
        arrived(wd, lsem.at[0])
        n_ctx = len(sent)

        def mid(slot):
            for q in (1, 2, 3):
                if q == 3 or slot in (1, 3):
                    take(ca, slot, q, cs_r)

            def one(nt, carry):
                c = aligned(nt * 256, 256, LANES)
                o = aligned(w.me * pc.w4 + nt * 256, 256, LANES)
                got = jnp.dot(ca[slot], wd[:, :, c].reshape(width, 256), preferred_element_type=F32)
                res = xa[slot, :, :, o].reshape(rows_b, 256).astype(F32)
                xm[slot, :, o] = (res + got).astype(BF16)
                return carry
            lax.fori_loop(0, pc.w4 // 256, one, 0)
            spread(xm, slot, ms_s, ms_r)

        mid(3)
        mid(1)
        mid(2)
        relay(xm, 1, 2, ms_s, ms_r)
        mid(0)
        relay(xm, 3, 2, ms_s, ms_r)
        relay(xm, 3, 1, ms_s, ms_r)
        relay(xm, 1, 1, ms_s, ms_r)
        for cp in sent[:n_ctx]:
            cp.wait_send()
        del sent[:n_ctx]
        for slot in (0, 2, 1, 3):
            for q in (1, 2, 3):
                if q == 3 or slot in (0, 2):
                    take(xm, slot, q, ms_r)
            norm_into(h2, slot, lambda rows, i, slot=slot: xm[slot, rows, :], g2_ref)

        gate_w = pc.gu_w // 2
        for b in range(4):
            load(2 + b, wg, lsem.at[b % 2])
            arrived(wg, lsem.at[b % 2])

            def one(j, carry):
                s, nt = j // (gate_w // 256), j % (gate_w // 256)
                act = h2[pl.ds(2 * s, 2)].reshape(2 * rows_b, width)
                gate = jnp.dot(act, wg[:, :, aligned(nt * 256, 256, LANES)].reshape(width, 256), preferred_element_type=F32)
                up = jnp.dot(act, wg[:, :, aligned(gate_w + nt * 256, 256, LANES)].reshape(width, 256), preferred_element_type=F32)
                val = (jax.nn.silu(gate) * up).astype(BF16)
                mm[pl.ds(2 * s, 2), :, aligned(b * gate_w + nt * 256, 256, LANES)] = val.reshape(2, rows_b, 256)
                return carry
            lax.fori_loop(0, 2 * (gate_w // 256), one, 0)

        h0, h1 = pl.ds(0, half), pl.ds(half, half)
        first_sends, home = {}, []

        def phase1(n):
            load(last_gu + 1 + n, wd, lsem.at[n % 2])
            for old in first_sends.get(n - 2, ()):
                old.wait_send()
            arrived(wd, lsem.at[n % 2])
            par = n % 2

            def one(j, carry):
                s, nt = j // (pc.dn_w // 256), j % (pc.dn_w // 256)
                c = aligned(nt * 256, 256, LANES)
                act = mm[pl.ds(2 * s, 2)].reshape(2 * rows_b, mm.shape[2])
                got = jnp.dot(act, wd[:, :, c].reshape(mm.shape[2], 256), preferred_element_type=F32)
                pp[par, pl.ds(2 * s, 2), :, c] = got.reshape(2, rows_b, 256)
                return carry
            lax.fori_loop(0, 2 * (pc.dn_w // 256), one, 0)
            first_sends[n] = []
            for path, dev, cc, rels in ((0, x, h0, (2, 3)), (1, y, h1, (1, 3))):
                for j, rel in enumerate(rels):
                    cp = remote(pp.at[par, rel, :, cc], r1.at[n, path, j], p1_s.at[n, path, j], p1_r.at[n, path, j], dev)
                    cp.start()
                    first_sends[n].append(cp)

        def phase2(n):
            par = n % 2
            for path, dev, cc, rel in ((0, y, h0, 1), (1, x, h1, 2)):
                arrived(r1.at[n, path, 1], p1_r.at[n, path, 1])
                r1[n, path, 1] = pp[par, rel, :, cc] + r1[n, path, 1]
                go(remote(r1.at[n, path, 1], r2.at[n, path], p2_s.at[n, path], p2_r.at[n, path], dev))
            for path, cc in ((0, h0), (1, h1)):
                arrived(r1.at[n, path, 0], p1_r.at[n, path, 0])
                r1[n, path, 0] = pp[par, 0, :, cc] + r1[n, path, 0]

        def phase3(n):
            for path in range(2):
                arrived(r2.at[n, path], p2_r.at[n, path])
                c = pl.ds(n * pc.dn_w + path * half, half)
                total = xm[0, :, c].astype(F32) + (r1[n, path, 0] + r2[n, path])
                xm[0, :, c] = total.astype(BF16)
            c = pl.ds(n * pc.dn_w, pc.dn_w)
            go(remote(xm.at[0, pl.ds(seq, seq), c], out_ref.at[:, c], o_s.at[n], o_r.at[n], w.partner()))
            cp = pltpu.make_async_copy(xm.at[0, pl.ds(0, seq), c], out_ref.at[:, c], o_l.at[n])
            cp.start()
            home.append(cp)

        for cp in sent:
            cp.wait_send()
        sent.clear()
        for n in range(4):
            phase1(n)
            if n >= 1:
                phase2(n - 1)
            if n >= 2:
                phase3(n - 2)
        phase2(3)
        phase3(2)
        phase3(3)

        for cp in sent:
            cp.wait_send()
        for n in (2, 3):
            for cp in first_sends[n]:
                cp.wait_send()
        for cp in local_kv + home:
            cp.wait()
        for rel in (1, 2, 3):
            arrived(k_ref.at[:, pl.ds(0, kv4)], kv_r.at[rel, 0])
            arrived(v_ref.at[:, pl.ds(0, kv4)], kv_r.at[rel, 1])

    pl.when(w.c == 1)(stream)
    pl.when(w.c == 0)(compute)


def layer(side, pc, head_dim, x, q_all, own2, early, g1, g2, cos_tab, sin_tab):
    _, seq, width = x.shape
    rows_b = 2 * seq
    kv_width = 4 * pc.kv4
    n_chunk = len(pc.chunks)
    far = pc.n_fsdp // 4
    ff4 = pc.f4 * pc.n_fsdp
    half = pc.dn_w // 2
    hbm = pl.BlockSpec(memory_space=pl.ANY)
    vmem = pl.BlockSpec(memory_space=pltpu.VMEM)
    dma = pltpu.SemaphoreType.DMA
    return pl.pallas_call(
        functools.partial(layer_kernel, side, pc, head_dim),
        out_shape=(
            jax.ShapeDtypeStruct((seq, width), BF16),
            jax.ShapeDtypeStruct((seq, kv_width), BF16),
            jax.ShapeDtypeStruct((seq, kv_width), BF16),
            jax.ShapeDtypeStruct((pc.n_fsdp, pc.rows, pc.late), BF16)),
        in_specs=[hbm, hbm, hbm, hbm, vmem, vmem, vmem, vmem],
        out_specs=(hbm, hbm, hbm, hbm),
        scratch_shapes=[
            pltpu.VMEM((4, 2, seq, width), BF16),
            pltpu.VMEM((4, rows_b, width), BF16),
            pltpu.VMEM((4, rows_b, width), BF16),
            pltpu.VMEM((pc.n_fsdp, pc.rows, pc.gu_w), BF16),
            pltpu.VMEM((pc.n_fsdp, pc.rows, pc.dn_w), BF16),
            pltpu.VMEM((4, rows_b, max(ff4, width)), BF16),
            pltpu.VMEM((2, 4, rows_b, pc.dn_w), F32),
            pltpu.VMEM((4, 2, 2, rows_b, half), F32),
            pltpu.VMEM((4, 2, rows_b, half), F32),
            pltpu.VMEM((rows_b, pc.qkv), F32),
            pltpu.VMEM((4, rows_b, 2 * pc.kv4), BF16),
            dma((2,)),
            dma((6,)), dma((4, 2)),
            dma((4, 3)), dma((4, 3)),
            dma((4, 3)), dma((4, 3)),
            dma((4, 2, 2)), dma((4, 2)),
            dma((4, 2, 2)), dma((4, 2, 2)),
            dma((4, 2)), dma((4, 2)),
            dma((4,)), dma((4,)), dma((4,)),
            dma((n_chunk, 2, far + 1)), dma((n_chunk, 2, far + 1)), dma((n_chunk, 2, far + 1)), dma((n_chunk,)),
        ],
        compiler_params=pltpu.CompilerParams(collective_id=2, has_side_effects=True, vmem_limit_bytes=67043328),
        name='layer',
    )(x, q_all, own2, early, g1, g2, cos_tab, sin_tab)


def solution(mesh):
    batch_axes = ('dp', 'fsdp')
    row_spec = P('fsdp', None)
    n_dp = mesh.shape['dp']
    n_fsdp = mesh.shape['fsdp']
    side = math.isqrt(n_dp)

    def device_step(tokens, embed_table, norm_attn, w_qkv, w_out, norm_mlp, w_gate_up, w_down, rope_scale):
        seq = tokens.shape[1]
        shard_rows, width = embed_table.shape
        head_dim = 2 * rope_scale.shape[0]
        rows = w_out.shape[0]
        q_width = rows * n_fsdp
        kv_width = (w_qkv.shape[1] - q_width) // 2
        pc = Pieces(rows, q_width // 4, kv_width // 4, width // 4, w_down.shape[0] // 4, n_fsdp, width)

        gains = jnp.stack([norm_attn, norm_mlp]).astype(F32)
        ids, gains = gather_ids(side, n_fsdp, tokens, gains)
        ids = ids.reshape(-1) - lax.axis_index('fsdp') * shard_rows
        owned = (ids >= 0) & (ids < shard_rows)
        table_rows = gather_table(ids, owned, embed_table)
        g1 = gains[:, 0].reshape(1, width)
        g2 = gains[:, 1].reshape(1, width)

        freq_expo = jnp.arange(head_dim // 2, dtype=F32) * (2.0 / head_dim)
        inv_freq = 1.0 / (rope_scale * jnp.power(ROPE_THETA, freq_expo))
        angles = jnp.arange(seq, dtype=F32)[:, None] * inv_freq[None, :]
        cos_tab, sin_tab = jnp.cos(angles), jnp.sin(angles)
        reps = LANES // head_dim
        cos_tab = jnp.concatenate([cos_tab, cos_tab] * reps, axis=1)
        sin_tab = jnp.concatenate([-sin_tab, sin_tab] * reps, axis=1)

        x, q_all, own2, early = embed(side, pc, table_rows.reshape(n_fsdp // 2, 2, seq, width), w_qkv, w_out, w_gate_up, w_down)
        out, k, v, _ = layer(side, pc, head_dim, x, q_all, own2, early, g1, g2, cos_tab, sin_tab)
        heads = (1, seq, kv_width // head_dim, head_dim)
        return out[None], k.reshape(heads), v.reshape(heads)

    return jax.shard_map(
        device_step,
        mesh=mesh,
        in_specs=(P(batch_axes, None), row_spec, P('fsdp'), row_spec, row_spec, P('fsdp'), row_spec, row_spec, P(None)),
        out_specs=(P(batch_axes, None, None), P(batch_axes, None, None, None), P(batch_axes, None, None, None)),
        check_vma=False,
    )
```

time: 866 us -> 305 us (0.35)
  waiting for transfers between devices: 620 us -> 0 us
  Pallas kernels: 0 us -> 292 us
  local copies, waits for them, and re-layouts: 101 us -> 6.98 us
  blocking collectives: 60.8 us -> 0 us
  matrix products: 57.3 us -> 0 us
  between operations: 14 us -> 0.69 us
    all_gather x4 -> x0, waiting for transfers between devices: 587 us -> none  [gather_rows(): return lax.all_gather(weight, 'fsdp', axis=0, tiled=True)]
    pallas_call x0 -> x4, Pallas kernels: none -> 292 us  [the longest x1 162 us: layer(): pl.pallas_call(functools.partial(layer_kernel, side, pc, head_dim), out_s...]
    gather x1 -> x0, local copies, waits for them, and re-layouts: 101 us -> none  [device_step(): jnp.take(embed_table, jnp.clip(local_ids, 0, shard_rows - 1), axis=0)]
    all_gather x3 -> x0, blocking collectives: 60.8 us -> none  [the longest x2 38.1 us: gather_rows(): return lax.all_gather(weight, 'fsdp', axis=0, tiled=True)]
    dot_general x6 -> x0, matrix products: 57.3 us -> none  [the longest x1 26.2 us: decoder_layer(): jnp.einsum('bld,df->blf', normed_mlp, w_gate_up, preferred_element_type=j...]
    reduce_scatter x1 -> x0, waiting for transfers between devices: 30.2 us -> none  [device_step(): lax.psum_scatter(table_rows, 'fsdp', scatter_dimension=0, tiled=True)]
  transfers between devices with their start and end apart: 5 -> 0, of which waited for: 5 -> 0; matrix products, arithmetic and copies ran while one was open for 5% -> 0% of each run, Pallas kernels for 0% -> 0%
where the time goes in v2:
time: 305 us
  Pallas kernels  292 us (96%)
  local copies, waits for them, and re-layouts  6.98 us (2%)
  other arithmetic  5.06 us (2%)
    pallas_call x1, Pallas kernels, layer(): pl.pallas_call(functools.partial(layer_kernel, side, pc, head_dim), out_s...  162 us
    pallas_call x1, Pallas kernels, embed(): pl.pallas_call(functools.partial(embed_kernel, side, pc), out_shape=(jax....  73.7 us
    pallas_call x1, Pallas kernels, gather_table(): pl.pallas_call(functools.partial(gather_kernel, n_tok), out_shape=jax.Sha...  41.7 us
    pallas_call x1, Pallas kernels, gather_ids(): pl.pallas_call(functools.partial(ids_kernel, side, n_fsdp), out_shape=(ja...  15.2 us

profile of v2, /device:TPU:21, one launch (start us, length us, event | category | flops | bytes accessed | tf_op | source)
XLA Modules:
  0.0 304.8 jit_solution(4958178869710706568)
XLA Ops:
  0.6 0.7 multiply_divide_fusion
  1.3 1.2 maximum_convert_fusion.gain_ref
  2.6 15.2 %ids.1 = (s32[16,1,128]{2,1,0:T(1,128)}, f32[16,2,128]{2,1,0:T(2,128)}) custom-call(s32[1,128]{1,0:T(1,128)} %tok_ref.1, f32[2,128]{1,0:T(2,128)} %maximum_convert_fusion.gain_ref), custom_call_target="tpu_custom_call" | custom-call | tf_op jit(solution)/shard_map/ids/pallas_call | solution.py:92
  17.8 1.4 slice_bitcast_fusion
  19.2 0.7 broadcast_subtract_fusion
  19.9 0.7 fusion.13
  20.6 0.3 fusion.9
  20.9 0.8 pad_maximum_fusion
  21.7 0.4 copy.14
  22.1 0.6 fusion.2.tgt_ref
  22.7 41.7 %shard_map.112 = bf16[2048,2048]{1,0:T(8,128)(2,1)} custom-call(s32[2048]{0:T(1024)S(1)} %fusion.11.gid_ref, s32[2048,1]{1,0:T(8,128)S(1)} %fusion.2.tgt_ref, bf16[1002,8,2048]{2,1,0:T(8,128)(2,1)} %bitcast.17), custom_call_target="tpu_custom_call" | custom-call | flops 2147483648 | bytes 75497472 | tf_op jit(solution)/shard_map/pallas_call | solution.py:190
  64.4 73.7 %embed.1 = (bf16[2,128,2048]{2,1,0:T(8,128)(2,1)}, bf16[16,128,768]{2,1,0:T(8,128)(2,1)}, bf16[2,128,6656]{2,1,0:T(8,128)(2,1)}, bf16[2,2,128,1536]{3,2,1,0:T(8,128)(2,1)}) custom-call(bf16[8,2,128,2048]{3,2,1,0:T(8,128)(2,1)} %bitcast.16, bf16[128,3072]{1,0:T(8,128)(2,1)} %w_qkv.1, bf16[128,2048]{1,0:T(8,128)(2,1)} %w_out.1, bf16[128,16384]{1,0:T(8,128)(2,1)} %w_gu.1, ...), custom_call_target="tpu_custom_call" | custom-call | tf_op jit(solution)/shard_map/embed/pallas_call | solution.py:372
  138.1 161.5 %layer.1 = (bf16[128,2048]{1,0:T(8,128)(2,1)}, bf16[128,512]{1,0:T(8,128)(2,1)}, bf16[128,512]{1,0:T(8,128)(2,1)}, bf16[16,128,6656]{2,1,0:T(8,128)(2,1)}) custom-call(bf16[2,128,2048]{2,1,0:T(8,128)(2,1)} %get-tuple-element.13.x_ref, bf16[16,128,768]{2,1,0:T(8,128)(2,1)} %get-tuple-element.14.q_ref, bf16[2,128,6656]{2,1,0:T(8,128)(2,1)} %get-tuple-element.15.own_ref, ...), custom_call_target="tpu_custom_call" | custom-call | tf_op jit(solution)/shard_map/layer/pallas_call | solution.py:745
  299.6 1.7 copy.19
  301.3 1.7 copy.20
  302.9 1.9 copy.22
  (1 shorter events, 0.0 us)
